TPU v7x, 32 devices: a 4x4x1 block of a 4x4x8 slice. The times are simulated.
32 devices in a mesh: dp: 1 (over z), tp: 4 (over y), ep: 8 (over x, core).
Axes of the slice: x: 4, y: 4, z: 1, core: 2. Of those that a mesh axis runs over, the one named last changes fastest.
The devices are a block of a 4x4x8 slice.
Arguments:
- tokens_x: bfloat16 [16384, 2048], P(('dp', 'ep', 'tp'))
- expert_ids: int32 [16384, 6], P(('dp', 'ep', 'tp'))
- route_gate: float32 [16384, 6], P(('dp', 'ep', 'tp'))
- w_gate: bfloat16 [64, 2048, 1408], P('ep', None, 'tp')
- w_up: bfloat16 [64, 2048, 1408], P('ep', None, 'tp')
- w_down: bfloat16 [64, 1408, 2048], P('ep', 'tp')
Outputs:
- output: bfloat16 [16384, 2048], P(('dp', 'ep', 'tp'))
All inputs are finite; a program needn't handle non-finite values.
Results may differ from a plain program's by a relative error of at most 0.00122.
Values are sent between devices in bfloat16 or wider.
A program may use at most 768 MiB of HBM per device.

v0:
```python
import jax
import jax.numpy as jnp
from jax import lax
from jax.sharding import PartitionSpec as P, NamedSharding


def solution(mesh):
    ep_size = mesh.shape['ep']
    row_spec = P(('dp', 'ep', 'tp'), None)
    w_in_spec = P('ep', None, 'tp')
    w_out_spec = P('ep', 'tp', None)

    def local_moe(x_local, ids_local, gate_local, w_gate, w_up, w_down):
        e_local = w_gate.shape[0]
        x_all = lax.all_gather(x_local, ('ep', 'tp'), tiled=True)
        ids_all = lax.all_gather(ids_local, ('ep', 'tp'), tiled=True)
        gate_all = lax.all_gather(gate_local, ('ep', 'tp'), tiled=True)
        num_tok, top_k = ids_all.shape
        local_pairs = num_tok * top_k // ep_size
        expert_cap = local_pairs // e_local
        local_ids = ids_all.reshape(-1) - lax.axis_index('ep') * e_local
        is_local = (local_ids >= 0) & (local_ids < e_local)
        sort_order = jnp.argsort(jnp.where(is_local, local_ids, e_local), stable=True)[:local_pairs]
        tok_rows = sort_order // top_k
        gate_rows = gate_all.reshape(-1)[sort_order]
        x_rows = x_all[tok_rows].reshape(e_local, expert_cap, -1)
        h_gate = jnp.einsum('ecd,edf->ecf', x_rows, w_gate, preferred_element_type=jnp.float32)
        h_up = jnp.einsum('ecd,edf->ecf', x_rows, w_up, preferred_element_type=jnp.float32)
        hidden = (jax.nn.silu(h_gate) * h_up).astype(jnp.bfloat16)
        out_rows = jnp.einsum('ecf,efd->ecd', hidden, w_down, preferred_element_type=jnp.float32)
        out_rows = out_rows.reshape(local_pairs, -1) * gate_rows[:, None]
        partial_sum = jax.ops.segment_sum(out_rows, tok_rows, num_segments=num_tok)
        y_local = lax.psum_scatter(partial_sum, ('ep', 'tp'), scatter_dimension=0, tiled=True)
        return y_local.astype(jnp.bfloat16)

    return jax.shard_map(local_moe, mesh=mesh, in_specs=(row_spec, row_spec, row_spec, w_in_spec, w_in_spec, w_out_spec), out_specs=row_spec, check_vma=False)
```

profile of v0, /device:TPU:97, one launch (start us, length us, event | category | flops | bytes accessed | tf_op | source)
XLA Modules:
  0.0 1667.3 jit_solution(12930256834957903397)
XLA Ops:
  6.5 0.0 all-gather.2.cloned.1.call-start
  6.6 0.7 all-gather.2.cloned.1.call-update
  7.3 0.1 reduce-scatter.4.cloned.1.call-start
  7.4 34.5 %all_gather.11 = f32[16384,6]{0,1:T(8,128)S(1)} all-gather(f32[512,6]{0,1:T(8,128)} %param.8), channel_id=1, replica_groups=mesh['dp'=1,'tp'=4,'ep'=8] {'ep','tp'}, dimensions={0}, use_global_device_ids=true | all-gather | bytes 405504 | tf_op jit(solution)/shard_map/all_gather | solution.py:17
  41.8 5.3 copy.10
  47.1 8.0 reshape.15
  55.1 34.2 %all_gather.9 = s32[16384,6]{0,1:T(8,128)S(1)} all-gather(s32[512,6]{0,1:T(8,128)} %param.7), channel_id=1, replica_groups=mesh['dp'=1,'tp'=4,'ep'=8] {'ep','tp'}, dimensions={0}, use_global_device_ids=true | all-gather | bytes 405504 | tf_op jit(solution)/shard_map/all_gather | solution.py:16
  89.4 5.3 copy.9
  94.7 8.0 sub.17
  102.7 0.1 and_select_fusion
  102.8 61.9 %sort.17 = (s32[98304]{0:T(1024)}, s32[98304]{0:T(1024)S(1)}) sort(s32[98304]{0:T(1024)S(1)} %and_select_fusion, s32[98304]{0:T(1024)S(1)} %iota.4), dimensions={0}, to_apply=%region_0.1 | sort | flops 1671168 | bytes 1572864 | tf_op jit(solution)/shard_map/jit(argsort)/sort | solution.py:23
  164.7 0.1 fusion.8
  164.7 120.4 %gather_fusion.1 = f32[12288]{0:T(1024)} fusion(f32[98304]{0:T(1024)S(1)} %reshape.15, s32[12288]{0:T(1024)S(1)} %get-tuple-element.11), kind=kCustom, calls=%fused_computation.1 | custom fusion | bytes 147456 | tf_op jit(solution)/shard_map/gather | solution.py:25
  285.1 9.0 sort.18
  294.1 0.6 broadcast_clamp_fusion
  294.8 286.1 %gather_fusion = bf16[12288,2048]{1,0:T(8,128)(2,1)} fusion(bf16[16384,2048]{1,0:T(8,128)(2,1)} %all-gather.2.cloned.1.call-done, s32[12288]{0:T(1024)S(1)} %get-tuple-element.9), kind=kCustom, calls=%fused_computation | custom fusion | bytes 100712448 | tf_op jit(solution)/shard_map/gather | solution.py:26
  580.8 31.3 %fusion.12 = f32[8,1536,352]{1,2,0:T(8,128)} fusion(bf16[8,1536,2048]{2,1,0:T(8,128)(2,1)} %bitcast.14, bf16[8,2048,352]{1,2,0:T(8,128)(2,1)} %param.9), kind=kOutput, calls=%fused_computation.23 | convolution fusion | flops 17716740096 | bytes 79167488 | tf_op jit(solution)/shard_map/ecd,edf->ecf/dot_general | solution.py:27
  612.1 72.4 %fusion.6 = f32[8,1536,2048]{2,1,0:T(8,128)} fusion(bf16[8,352,2048]{2,1,0:T(8,128)(2,1)} %param.11, f32[8,1536,352]{1,2,0:T(8,128)} %fusion.12, bf16[8,1536,2048]{2,1,0:T(8,128)(2,1)} %bitcast.15, bf16[8,2048,352]{1,2,0:T(8,128)(2,1)} %param.10), kind=kOutput, calls=%fused_computation.9 | convolution fusion | flops 35459432448 | bytes 191365120 | tf_op jit(solution)/shard_map/ecf,efd->ecd/dot_general | solution.py:30
  684.5 0.0 copy-done
  684.5 66.4 %bitcast_multiply_fusion = f32[12288,2048]{1,0:T(8,128)} fusion(f32[8,1536,2048]{2,1,0:T(8,128)} %fusion.6, f32[12288]{0:T(1024)S(1)} %copy-done), kind=kLoop, calls=%fused_computation.6 | loop fusion | flops 25165824 | bytes 201375744 | tf_op jit(solution)/shard_map/mul | solution.py:31
  750.9 361.3 %scatter_custom_fusion = f32[16384,2048]{1,0:T(8,128)} fusion(s32[12288]{0:T(1024)} %get-tuple-element.7, f32[12288,2048]{1,0:T(8,128)} %bitcast_multiply_fusion, s32[12288]{0:T(1024)} %broadcast_clamp_fusion, f32[]{:T(128)} %constant.10.clone.1), kind=kCustom, calls=%fused_computation.4 | custom fusion | flops 25165824 | bytes 134218240 | tf_op jit(solution)/shard_map/scatter-add | solution.py:32
  1112.2 0.1 reduce-scatter.4.cloned.1.call-update
  1112.2 543.9 %reduce-scatter.4.cloned.1.call-done = f32[512,2048]{1,0:T(8,128)} async-done(((f32[16384,2048]{1,0:T(8,128)}), f32[512,2048]{1,0:T(8,128)}) %reduce-scatter.4.cloned.1.call-update) | async-done | bytes 4194320
  1656.2 3.8 convert_element_type.7
  (5 shorter events, 0.1 us)
Async XLA Ops:
  6.5 288.2 %all-gather.2.cloned.1.call-start = ((), (), s32[]{:S(2)}) async-start(), calls=%async_computation.1 | async-start | bytes 69206016 | tf_op jit(solution)/shard_map/all_gather | solution.py:15
  7.3 1648.8 %reduce-scatter.4.cloned.1.call-start = ((), (), s32[]{:S(2)}) async-start(), calls=%async_computation.2 | async-start | bytes 138412032
  612.1 72.4 %copy-start = (f32[12288]{0:T(1024)S(1)}, f32[12288]{0:T(1024)}, u32[]{:S(2)}) copy-start(f32[12288]{0:T(1024)} %gather_fusion.1) | copy-start | bytes 147460
Sparse Core Ops, SparseCore 0:
  9.4 202.9 all-gather.1
  1112.4 543.7 reduce-scatter.3
where the time goes:
time: 1680 us; the launch traced here: 1670 us
  waiting for transfers between devices  545 us (32%)
  other arithmetic  503 us (30%)
  local copies, waits for them, and re-layouts  433 us (26%)
  matrix products  104 us (6%)
  blocking collectives  68.7 us (4%)
    unnamed x3, waiting for transfers between devices  545 us
    scatter-add x3, other arithmetic, local_moe(): partial_sum = jax.ops.segment_sum(out_rows, tok_rows, num_segments=num_tok)  371 us
    gather x1, local copies, waits for them, and re-layouts, local_moe(): x_rows = x_all[tok_rows].reshape(e_local, expert_cap, -1)  286 us
    gather x1, local copies, waits for them, and re-layouts, local_moe(): gate_rows = gate_all.reshape(-1)[sort_order]  120 us
    dot_general x1, matrix products, local_moe(): jnp.einsum('ecf,efd->ecd', hidden, w_down, preferred_element_type=jnp.flo...  72.4 us
    mul x1, other arithmetic, local_moe(): out_rows = out_rows.reshape(local_pairs, -1) * gate_rows[:, None]  66.4 us
    sort x1, other arithmetic, local_moe(): jnp.argsort(jnp.where(is_local, local_ids, e_local), stable=True)  61.9 us
    all_gather x1, blocking collectives, local_moe(): gate_all = lax.all_gather(gate_local, ('ep', 'tp'), tiled=True)  34.5 us
  transfers between devices with their start and end apart: 2, of which 1 were waited for; matrix products, arithmetic and copies ran while one was open for 13% of the time, Pallas kernels for 0%

commit v1 on v0

v1 whole, which is shorter than its diff:
```python
import functools

import jax
import jax.numpy as jnp
from jax import lax
from jax.experimental import pallas as pl
from jax.experimental.pallas import tpu as pltpu
from jax.sharding import PartitionSpec as P

MESH = pl.DeviceIdType.MESH
CHUNKS = 4
BF16 = jnp.bfloat16
F32 = jnp.float32

S, A, B, O = 0, 1, 2, 3


def order_of(i):
    t = i + (i + 13) // 16 + 3 * (i // 15)
    p, r = t // 4, t % 4
    return r + r // 2 - 2 * (r // 3), p - r // 3


BATCH = {order_of(i): i for i in range(16)}


def place(y, q):
    high, low = y // 2, y % 2
    return 2 * ((high + q // 2) % 2) + (low + (q + 1) // 2) % 2


def routing_tables(ids, gates, experts, per_expert):
    rows = ids.shape[0]
    chosen = ids[:, :, None] == jnp.arange(experts, dtype=ids.dtype)
    picked = jnp.any(chosen, axis=1)
    weight = jnp.sum(jnp.where(chosen, gates[:, :, None], 0.0), axis=1)
    before = (jnp.arange(rows)[:, None] > jnp.arange(rows)[None, :]).astype(BF16)
    rank = jnp.dot(before, picked.astype(BF16), preferred_element_type=F32)
    rank = jnp.where(picked, rank, -1.0)
    hit = rank[:, :, None] == jnp.arange(per_expert, dtype=F32)
    row = jnp.arange(rows, dtype=F32)[:, None, None]
    position = jnp.sum(jnp.where(hit, row, 0.0), axis=0)
    value = jnp.sum(jnp.where(hit, weight[:, :, None], 0.0), axis=0)
    return position, value


def moe_kernel(nx, ny, x_ref, meta_ref, wg_ref, wu_ref, wd_ref, out_ref, tok_ref, h_ref, w_ref, db_ref,
               metav, rb, ms, mr, ty_s, ty_r, tx_s, tx_r, td_s, td_r, hd_r, hf_s, hf_r, wa_s, wa_r, wb_s, wb_r, wf_s, wf_r,
               rs_r, db_r, of_r):
    rows, width = x_ref.shape
    half = rows // 2
    el, _, ff = wg_ref.shape
    per = h_ref.shape[5]
    pairs = el * per
    kc, cw = w_ref.shape[0], w_ref.shape[4]
    eps = 2 * nx
    y = lax.axis_index('tp')
    ep = lax.axis_index('ep')
    x, c = ep // 2, ep % 2
    ya, yb, yo = place(y, A), place(y, B), place(y, O)
    yq = (y, ya, yb, yo)
    xp, xm = (x + 1) % nx, (x + nx - 1) % nx
    colb = ((y + y // 2) % 2) * (kc * cw)
    cola = ((ya + ya // 2) % 2) * (kc * cw)
    me = y * eps + ep

    dev_a = {'tp': ya, 'ep': ep}
    dev_b = {'tp': yb, 'ep': ep}
    dev_p = {'tp': y, 'ep': 2 * x + 1 - c}
    dev_xp = {'tp': y, 'ep': 2 * xp + c}
    dev_xm = {'tp': y, 'ep': 2 * xm + c}

    def remote(src, dst, send, recv, dev):
        return pltpu.make_async_remote_copy(src_ref=src, dst_ref=dst, send_sem=send, recv_sem=recv, device_id=dev, device_id_type=MESH)

    def lin(xs, ys, cs):
        return ys * eps + 2 * xs + cs

    barrier = pltpu.get_barrier_semaphore()

    def peer_of(d):
        other = (me + d) % (ny * eps)
        return other // eps, other % eps

    def greet(d, carry):
        py, pe = peer_of(d)
        pl.semaphore_signal(barrier, inc=1, device_id={'tp': py, 'ep': pe}, device_id_type=MESH)
        return carry

    lax.fori_loop(1, ny * eps, greet, 0)
    pl.semaphore_wait(barrier, ny * eps - 1)

    def meta_copy(d):
        py, pe = peer_of(d)
        return remote(meta_ref.at[pe], metav.at[me], ms.at[d], mr.at[me], {'tp': py, 'ep': pe})

    def meta_send(d, carry):
        meta_copy(d).start()
        return carry

    lax.fori_loop(1, ny * eps, meta_send, 0)
    metav[me] = meta_ref[ep]

    def own(dxm, q):
        return tok_ref.at[(x + dxm) % nx, yq[q], c]

    def rows_of(ref, part):
        return ref.at[pl.ds(part * half, half)]

    def ty(n):
        if n == 0:
            return remote(x_ref, tok_ref.at[x, y, c], ty_s.at[0], ty_r.at[0], dev_a)
        if n == 1:
            return remote(x_ref, tok_ref.at[x, y, c], ty_s.at[1], ty_r.at[1], dev_b)
        if n == 2:
            return remote(rows_of(own(0, B), 0), rows_of(own(0, B), 0), ty_s.at[2], ty_r.at[2], dev_a)
        return remote(rows_of(own(0, A), 1), rows_of(own(0, A), 1), ty_s.at[3], ty_r.at[3], dev_b)

    def tx(q, n):
        if n < 2:
            src = x_ref if q == S else own(0, q)
            return remote(src, own(0, q), tx_s.at[q, n], tx_r.at[q, n], (dev_xp, dev_xm)[n])
        block = rows_of(own((3, 1)[n - 2], q), n - 2)
        return remote(block, block, tx_s.at[q, n], tx_r.at[q, n], (dev_xp, dev_xm)[n - 2])

    def td(q, dxm):
        src = x_ref if (q == S and dxm == 0) else own(dxm, q)
        return remote(src, own(dxm, q), td_s.at[q, dxm], td_r.at[q, dxm], dev_p)

    def wa(k):
        src = wd_ref.at[:, :, pl.ds(pl.multiple_of(cola + k * cw, cw), cw)]
        return remote(src, w_ref.at[k, y], wa_s.at[k], wa_r.at[k], dev_a)

    def wb(k):
        src = wd_ref.at[:, :, pl.ds(pl.multiple_of(colb + k * cw, cw), cw)]
        return remote(src, w_ref.at[k, y], wb_s.at[k], wb_r.at[k], dev_b)

    def wf(k):
        return remote(w_ref.at[k, ya], w_ref.at[k, ya], wf_s.at[k], wf_r.at[k], dev_b)

    def forward_w(k):
        wa(k).wait_recv()
        wf(k).start()

    def hf(i):
        dxm, q = order_of(i)
        block = h_ref.at[yb, (x + dxm) % nx, place(yb, q)]
        return remote(block, block, hf_s.at[i], hf_r.at[i], dev_a)

    def hd_wait(i):
        block = h_ref.at[0, 0, 0]
        remote(block, block, hf_s.at[i], hd_r.at[i], dev_a).wait_recv()

    def forward_h(i):
        hd_wait(i)
        hf(i).start()

    for n in (0, 1):
        ty(n).start()
        tx(S, n).start()
    td(S, 0).start()
    wa(0).start()
    wb(0).start()

    def comm(step):
        if step == 1:
            ty(0).wait_recv()
            ty(1).wait_recv()
            ty(2).start()
            ty(3).start()
            tx(A, 0).start()
            tx(A, 1).start()
            td(A, 0).start()
            td(B, 0).start()
            for n in (0, 1):
                tx(S, n).wait_recv()
            for n in (2, 3):
                tx(S, n).start()
            td(S, 3).start()
            td(S, 1).start()
            tx(B, 0).start()
            tx(B, 1).start()
        if step == 4:
            for n in (0, 1):
                tx(A, n).wait_recv()
            for n in (2, 3):
                tx(A, n).start()
            td(A, 3).start()
            td(A, 1).start()
            ty(2).wait_recv()
            ty(3).wait_recv()
            td(O, 0).start()
            tx(O, 0).start()
            tx(O, 1).start()
            forward_w(0)
            wb(1).start()
        if step in (6, 10, 14, 15):
            q = {6: S, 10: A, 14: B, 15: O}[step]
            tx(q, 2).wait_recv()
            tx(q, 3).wait_recv()
            td(q, 2).start()
        if step in (8, 12):
            q = {8: B, 12: O}[step]
            for n in (0, 1):
                tx(q, n).wait_recv()
            for n in (2, 3):
                tx(q, n).start()
            td(q, 3).start()
            td(q, 1).start()
        if step == 8:
            wa(1).start()
        for i in {10: (7,), 12: (8, 9), 14: (11,), 15: (12, 13)}.get(step, ()):
            forward_h(i)
        if step == 12:
            forward_w(1)
            wb(2).start()
        if step == 15:
            wa(2).start()

    row_id = lax.broadcasted_iota(jnp.int32, (rows, pairs), 0)

    def one_hot(src):
        pos = metav[src, 0:1, :].astype(jnp.int32)
        return (row_id == pos).astype(F32).astype(BF16)

    def meta_wait(src):
        remote(meta_ref.at[0], metav.at[src], ms.at[0], mr.at[src], dev_p).wait_recv()

    def phase_one(wg, wu, tb, xg, hb, wl, tl, hl, hd_s):
        load_g = pltpu.make_async_copy(wg_ref, wg, wl.at[0])
        load_u = pltpu.make_async_copy(wu_ref, wu, wl.at[1])
        load_g.start()
        load_u.start()

        def hidden_out(i, dxm, q, slot):
            xs, ys = (x + dxm) % nx, place(y, q)
            return (
                pltpu.make_async_copy(hb.at[slot], h_ref.at[y, xs, ys], hl.at[slot]),
                remote(hb.at[slot], h_ref.at[y, xs, ys], hd_s.at[slot], hd_r.at[i], dev_a),
                remote(hb.at[slot], h_ref.at[y, xs, ys], hd_s.at[slot], hd_r.at[i], dev_b),
            )

        def drain(i):
            dxm, q = order_of(i)
            local, _, away = hidden_out(i, dxm, q, i % 2)

            @pl.when(q < 2)
            def _():
                local.wait()

            away.wait_send()

        def batch(i, carry):
            for step in (1, 4, 6, 8, 10, 12, 14, 15):
                pl.when(i == step)(functools.partial(comm, step))
            dxm, q = order_of(i)
            xs, ys = (x + dxm) % nx, place(y, q)
            slot = i % 2
            remote(tok_ref.at[xs, ys, c], tok_ref.at[xs, ys, c], td_s.at[q, dxm], td_r.at[q, dxm], dev_p).wait_recv()
            mine = pltpu.make_async_copy(x_ref, tb.at[0], tl.at[0])
            other = pltpu.make_async_copy(tok_ref.at[xs, ys, c], tb.at[0], tl.at[0])
            theirs = pltpu.make_async_copy(tok_ref.at[xs, ys, 1 - c], tb.at[1], tl.at[1])

            @pl.when(i == 0)
            def _():
                mine.start()

            @pl.when(i > 0)
            def _():
                other.start()

            theirs.start()

            @pl.when(i > 0)
            def _():
                meta_wait(lin(xs, ys, c))

            meta_wait(lin(xs, ys, 1 - c))

            @pl.when(i == 0)
            def _():
                load_g.wait()
                load_u.wait()

            @pl.when(i > 1)
            def _():
                drain(i - 2)

            for s in (0, 1):
                (other, theirs)[s].wait()
                hot = one_hot(lin(xs, ys, c if s == 0 else 1 - c))
                step = min(512, width)
                for lo in range(0, width, step):
                    got = lax.dot_general(hot, tb[s, :, lo:lo + step], (((0,), (0,)), ((), ())), preferred_element_type=F32)
                    xg[:, s, :, lo:lo + step] = got.astype(BF16).reshape(el, per, step)

            def expert(e, carry):
                lhs = xg[e].reshape(2 * per, width)
                a = jnp.dot(lhs, wg[e], preferred_element_type=F32)
                b = jnp.dot(lhs, wu[e], preferred_element_type=F32)
                hid = (a * jax.nn.sigmoid(a) * b).astype(BF16).reshape(2, per, ff)
                for s in (0, 1):
                    hb[slot, jnp.where(c == s, 0, 1), e] = hid[0] if s == 0 else hid[1]
                return carry

            lax.fori_loop(0, el, expert, 0)
            local, to_a, to_b = hidden_out(i, dxm, q, slot)

            @pl.when(q < 2)
            def _():
                local.start()
                to_a.start()

            @pl.when(q >= 2)
            def _():
                to_b.start()

            return carry

        lax.fori_loop(0, 16, batch, 0)
        drain(14)
        drain(15)

    pl.run_scoped(
        phase_one,
        pltpu.VMEM((el, width, ff), BF16),
        pltpu.VMEM((el, width, ff), BF16),
        pltpu.VMEM((2, rows, width), BF16),
        pltpu.VMEM((el, 2, per, width), BF16),
        pltpu.VMEM((2, 2, el, per, ff), BF16),
        pltpu.SemaphoreType.DMA((2,)),
        pltpu.SemaphoreType.DMA((2,)),
        pltpu.SemaphoreType.DMA((2,)),
        pltpu.SemaphoreType.DMA((2,)),
    )
    wa(3).start()
    wb(3).start()
    forward_h(14)
    forward_h(15)

    def unit_of(n):
        return 2 * (n // 8) + n % 2, (n % 8) // 2

    def phase_two(wv, hv, gc, o3, pb, pp, sb, dv, fb, wl, hvl, dl, pp_s, rs_s, of_s, ol):
        def shape_of(n):
            k, j = unit_of(n)
            return k, j, ((x + 2 * nx - 1 - j) % nx, (x + 1 + j) % nx), (y, ya)

        def load_w(k):
            src = wd_ref.at[:, :, pl.ds(pl.multiple_of(colb + k * cw, cw), cw)]
            copies = [pltpu.make_async_copy(src, wv.at[k % 2, S], wl.at[S])]
            for q in (A, B, O):
                copies.append(pltpu.make_async_copy(w_ref.at[k, yq[q]], wv.at[k % 2, q], wl.at[q]))
            return copies

        def partner_copy(n, d):
            k, j, _, _ = shape_of(n)
            return remote(pp.at[n % 2, d], db_ref.at[d, k, j], pp_s.at[n % 2, d], db_r.at[d, k, j], dev_p)

        def ring_copy(n, d, k, j):
            return remote(sb.at[n % 4, d], rb.at[d, k, j], rs_s.at[n % 4, d], rs_r.at[d, k, j], (dev_xp, dev_xm)[d])

        def out_copies(n, k):
            cols = out_ref.at[:, pl.ds(pl.multiple_of(colb + k * cw, cw), cw)]
            return (
                pltpu.make_async_copy(fb.at[n % 2, 0], cols, ol.at[n % 2]),
                remote(fb.at[n % 2, 1], cols, of_s.at[n % 2], of_r.at[k], dev_a),
            )

        def make(n):
            k, j, xs, ys = shape_of(n)
            for step in range(4):
                @pl.when(n == 2 * step)
                def _(step=step):
                    minus, plus = (3 - step) % 4, (1 + step) % 4
                    hd_wait(BATCH[(minus, A)])
                    hd_wait(BATCH[(plus, S)])
                    for i in (BATCH[(minus, O)], BATCH[(plus, B)]):
                        hf(i).wait_recv()

            @pl.when(n == 4)
            def _():
                forward_w(2)

            @pl.when(n == 6)
            def _():
                forward_w(3)

            for kk, at in ((0, 0), (1, 1), (2, 8), (3, 9)):
                @pl.when(n == at)
                def _(kk=kk):
                    wb(kk).wait_recv()
                    wf(kk).wait_recv()
                    copies = load_w(kk)
                    for copy in copies:
                        copy.start()
                    for copy in copies:
                        copy.wait()

            @pl.when(n % 2 == 0)
            def _():
                copies = []
                for d in (0, 1):
                    for rel in (0, 1):
                        cs = c if rel == 0 else 1 - c
                        for q in (S, A, B, O):
                            copies.append(pltpu.make_async_copy(
                                h_ref.at[yq[q], xs[d], ys[d], cs], hv.at[q, :, 2 * d + rel], hvl.at[q, 2 * d + rel]))
                for copy in copies:
                    copy.start()
                for d in (0, 1):
                    for rel in (0, 1):
                        gate = metav[lin(xs[d], ys[d], c if rel == 0 else 1 - c), 1:2, :]
                        gc[:, 2 * d + rel] = jnp.transpose(jnp.broadcast_to(gate, (gc.shape[3], pairs))).reshape(el, per, gc.shape[3])
                for copy in copies:
                    copy.wait()

            def expert(e, carry):
                o = jnp.zeros((4 * per, cw), F32)
                for q in (S, A, B, O):
                    o = o + jnp.dot(hv[q, e].reshape(4 * per, ff), wv[k % 2, q, e], preferred_element_type=F32)
                g = gc[e].reshape(4 * per, gc.shape[3])
                v = o * jnp.concatenate([g] * (cw // gc.shape[3]), axis=1)
                hi = v.astype(BF16)
                rest = v - hi.astype(F32)
                mid = rest.astype(BF16)
                low = (rest - mid.astype(F32)).astype(BF16)
                o3[:, 0, e] = hi.reshape(4, per, cw)
                o3[:, 1, e] = mid.reshape(4, per, cw)
                o3[:, 2, e] = low.reshape(4, per, cw)
                return carry

            lax.fori_loop(0, el, expert, 0)

            @pl.when(n >= 2)
            def _():
                for d in (0, 1):
                    partner_copy(n - 2, d).wait_send()

            for rel in (1, 0):
                for d in (0, 1):
                    hot = one_hot(lin(xs[d], ys[d], c if rel == 0 else 1 - c))
                    total = jnp.dot(hot, o3[2 * d + rel, 0].reshape(pairs, cw), preferred_element_type=F32)
                    total += jnp.dot(hot, o3[2 * d + rel, 1].reshape(pairs, cw), preferred_element_type=F32)
                    total += jnp.dot(hot, o3[2 * d + rel, 2].reshape(pairs, cw), preferred_element_type=F32)
                    if rel == 1:
                        pp[n % 2, d] = total
                        partner_copy(n, d).start()
                    else:
                        pb[n % 2, d] = total

        def join(n):
            k, j, _, _ = shape_of(n)
            loads = [pltpu.make_async_copy(db_ref.at[d, k, j], dv.at[d], dl.at[d]) for d in (0, 1)]
            for d in (0, 1):
                partner_copy(n, d).wait_recv()
                loads[d].start()

            @pl.when((j < 3) & (n >= 4))
            def _():
                for d in (0, 1):
                    ring_copy(n, d, k, j).wait_send()

            @pl.when((j == 3) & (n >= 8))
            def _():
                local, away = out_copies(n, k)
                local.wait()
                away.wait_send()

            for d in (0, 1):
                loads[d].wait()

                @pl.when(j == 0)
                def _():
                    sb[n % 4, d] = pb[n % 2, d] + dv[d]

                @pl.when((j > 0) & (j < 3))
                def _():
                    ring_copy(n, d, k, j - 1).wait_recv()
                    sb[n % 4, d] = pb[n % 2, d] + dv[d] + rb[d, k, j - 1]

                @pl.when(j == 3)
                def _():
                    ring_copy(n, d, k, j - 1).wait_recv()
                    fb[n % 2, d] = (pb[n % 2, d] + dv[d] + rb[d, k, j - 1]).astype(BF16)

                @pl.when(j < 3)
                def _():
                    ring_copy(n, d, k, j).start()

            @pl.when(j == 3)
            def _():
                local, away = out_copies(n, k)
                local.start()
                away.start()

        def unit(n, carry):
            @pl.when(n < 4 * kc)
            def _():
                make(n)

            @pl.when(n > 0)
            def _():
                join(n - 1)

            return carry

        lax.fori_loop(0, 4 * kc + 1, unit, 0)
        for d in (0, 1):
            for n in (14, 15):
                partner_copy(n, d).wait_send()
            for n in (10, 11, 12, 13):
                ring_copy(n, d, 0, 0).wait_send()
        for n in (14, 15):
            local, away = out_copies(n, n - 12)
            local.wait()
            away.wait_send()
        for k in range(kc):
            out_copies(0, k)[1].wait_recv()

    lane = min(128, cw)
    pl.run_scoped(
        phase_two,
        pltpu.VMEM((2, 4, el, ff, cw), BF16),
        pltpu.VMEM((4, el, 4, per, ff), BF16),
        pltpu.VMEM((el, 4, per, lane), F32),
        pltpu.VMEM((4, 3, el, per, cw), BF16),
        pltpu.VMEM((2, 2, rows, cw), F32),
        pltpu.VMEM((2, 2, rows, cw), F32),
        pltpu.VMEM((4, 2, rows, cw), F32),
        pltpu.VMEM((2, rows, cw), F32),
        pltpu.VMEM((2, 2, rows, cw), BF16),
        pltpu.SemaphoreType.DMA((4,)),
        pltpu.SemaphoreType.DMA((4, 4)),
        pltpu.SemaphoreType.DMA((2,)),
        pltpu.SemaphoreType.DMA((2, 2)),
        pltpu.SemaphoreType.DMA((4, 2)),
        pltpu.SemaphoreType.DMA((2,)),
        pltpu.SemaphoreType.DMA((2,)),
    )

    def meta_done(d, carry):
        meta_copy(d).wait_send()
        return carry

    lax.fori_loop(1, ny * eps, meta_done, 0)
    for n in range(4):
        ty(n).wait_send()
    for q in (S, A, B, O):
        for n in range(4):
            tx(q, n).wait_send()
        for dxm in range(4):
            td(q, dxm).wait_send()
    for k in range(kc):
        wa(k).wait_send()
        wb(k).wait_send()
        wf(k).wait_send()
    for i in (7, 8, 9, 11, 12, 13, 14, 15):
        hf(i).wait_send()


def solution(mesh):
    ny, eps = mesh.shape['tp'], mesh.shape['ep']
    nx = eps // 2
    row_spec = P(('dp', 'ep', 'tp'), None)
    w_in_spec = P('ep', None, 'tp')
    w_out_spec = P('ep', 'tp', None)

    def local_moe(x, ids, gates, w_gate, w_up, w_down):
        rows, width = x.shape
        el, _, ff = w_gate.shape
        experts = el * eps
        per = rows * ids.shape[1] // experts
        pairs = el * per
        cw = width // 2 // CHUNKS
        position, value = routing_tables(ids, gates, experts, per)
        meta = jnp.stack([position.reshape(eps, pairs), value.reshape(eps, pairs)], axis=1)
        meta = jnp.pad(meta, ((0, 0), (0, 6), (0, 0)))
        hbm = pl.BlockSpec(memory_space=pl.ANY)
        vmem = pl.BlockSpec(memory_space=pltpu.VMEM)
        dma = pltpu.SemaphoreType.DMA
        outs = pl.pallas_call(
            functools.partial(moe_kernel, nx, ny),
            name='moe_kernel',
            out_shape=[
                jax.ShapeDtypeStruct((rows, width), BF16),
                jax.ShapeDtypeStruct((nx, ny, 2, rows, width), BF16),
                jax.ShapeDtypeStruct((ny, nx, ny, 2, el, per, ff), BF16),
                jax.ShapeDtypeStruct((CHUNKS, ny, el, ff, cw), BF16),
                jax.ShapeDtypeStruct((2, CHUNKS, 4, rows, cw), F32),
            ],
            in_specs=[hbm, vmem, hbm, hbm, hbm],
            out_specs=[hbm] * 5,
            scratch_shapes=[
                pltpu.VMEM((ny * eps, 8, pairs), F32),
                pltpu.VMEM((2, CHUNKS, 3, rows, cw), F32),
                dma((ny * eps,)), dma((ny * eps,)),
                dma((4,)), dma((4,)),
                dma((4, 4)), dma((4, 4)),
                dma((4, 4)), dma((4, 4)),
                dma((16,)), dma((16,)), dma((16,)),
                dma((CHUNKS,)), dma((CHUNKS,)), dma((CHUNKS,)), dma((CHUNKS,)), dma((CHUNKS,)), dma((CHUNKS,)),
                dma((2, CHUNKS, 3)), dma((2, CHUNKS, 4)), dma((CHUNKS,)),
            ],
            compiler_params=pltpu.CompilerParams(collective_id=0, has_side_effects=True, vmem_limit_bytes=66 * 1000 * 1000),
        )(x, meta, w_gate, w_up, w_down)
        return outs[0]

    return jax.shard_map(
        local_moe, mesh=mesh, in_specs=(row_spec, row_spec, row_spec, w_in_spec, w_in_spec, w_out_spec),
        out_specs=row_spec, check_vma=False)
```

time: 1680 us -> 663 us (0.39)
  Pallas kernels: 0 us -> 622 us
  waiting for transfers between devices: 545 us -> 0 us
  other arithmetic: 503 us -> 3.63 us
  local copies, waits for them, and re-layouts: 433 us -> 35 us
  matrix products: 104 us -> 0.27 us
  blocking collectives: 68.7 us -> 0 us
    pallas_call x0 -> x1, Pallas kernels: none -> 622 us  [local_moe(): pl.pallas_call(functools.partial(moe_kernel, nx, ny), name='moe_kernel',...]
    unnamed x3 -> x0, waiting for transfers between devices: 545 us -> none
    gather x2 -> x0, local copies, waits for them, and re-layouts: 406 us -> none  [the longest x1 286 us: local_moe(): x_rows = x_all[tok_rows].reshape(e_local, expert_cap, -1)]
    scatter-add x3 -> x0, other arithmetic: 371 us -> none  [local_moe(): partial_sum = jax.ops.segment_sum(out_rows, tok_rows, num_segments=num_tok)]
    dot_general x2 -> x1, matrix products: 104 us -> 0.27 us  [routing_tables(): rank = jnp.dot(before, picked.astype(BF16), preferred_element_type=F32)]
    all_gather x2 -> x0, blocking collectives: 68.7 us -> none  [the longest x1 34.5 us: local_moe(): gate_all = lax.all_gather(gate_local, ('ep', 'tp'), tiled=True)]
    mul x1 -> x0, other arithmetic: 66.4 us -> none  [local_moe(): out_rows = out_rows.reshape(local_pairs, -1) * gate_rows[:, None]]
    sort x1 -> x0, other arithmetic: 61.9 us -> none  [local_moe(): jnp.argsort(jnp.where(is_local, local_ids, e_local), stable=True)]
  transfers between devices with their start and end apart: 2 -> 0, of which waited for: 1 -> 0; matrix products, arithmetic and copies ran while one was open for 13% -> 0% of each run, Pallas kernels for 0% -> 0%
where the time goes in v1:
time: 663 us; the launch traced here: 661 us
  Pallas kernels  622 us (94%)
  local copies, waits for them, and re-layouts  35 us (5%)
    pallas_call x1, Pallas kernels, local_moe(): pl.pallas_call(functools.partial(moe_kernel, nx, ny), name='moe_kernel',...  622 us
    unnamed x3, local copies, waits for them, and re-layouts  34.8 us

profile of v1, /device:TPU:97, one launch (start us, length us, event | category | flops | bytes accessed | tf_op | source)
XLA Modules:
  0.0 660.9 jit_solution(11478744451102278804)
XLA Ops:
  0.0 0.8 fusion
  0.8 0.3 convolution_select_fusion
  1.1 0.8 select_reduce_fusion.2
  1.9 1.3 select_reduce_fusion.1
  3.3 0.1 stack_reshape.8
  3.3 0.1 stack_reshape.9
  3.4 0.7 select_maximum_fusion.meta_ref
  4.1 16.2 %copy.21.wg_ref = bf16[8,2048,352]{2,1,0:T(8,128)(2,1)} copy(bf16[8,2048,352]{1,2,0:T(8,128)(2,1)} %param.9) | data formatting | bytes 23068672 | tf_op args[3]
  20.3 15.4 %copy.22.wu_ref = bf16[8,2048,352]{2,1,0:T(8,128)(2,1)} copy(bf16[8,2048,352]{1,2,0:T(8,128)(2,1)} %param.10) | data formatting | bytes 23068672 | tf_op args[4]
  35.8 622.0 %moe_kernel.1 = (bf16[512,2048]{1,0:T(8,128)(2,1)}, bf16[4,4,2,512,2048]{4,3,2,1,0:T(8,128)(2,1)}, bf16[4,4,4,2,8,48,352]{6,5,4,3,2,1,0:T(8,128)(2,1)}, bf16[4,4...) custom-call(bf16[512,2048]{1,0:T(8,128)(2,1)} %x_ref.1, f32[8,8,384]{2,1,0:T(8,128)} %select_maximum_fusion.meta_ref, ...), custom_call_target="tpu_custom_call" | custom-call | tf_op jit(solution)/shard_map/moe_kernel/pallas_call | solution.py:582
  657.7 3.2 copy.24

commit v2 on v1

v2 whole, which is shorter than its diff:
```python
import functools

import jax
import jax.numpy as jnp
from jax import lax
from jax.experimental import pallas as pl
from jax.experimental.pallas import tpu as pltpu
from jax.sharding import PartitionSpec as P

MESH = pl.DeviceIdType.MESH
CHUNKS = 4
PIECES = 2
BF16 = jnp.bfloat16
F32 = jnp.float32

S, A, B, O = 0, 1, 2, 3

UNITS = ((3, 0), (2, 0), (2, 1), (3, 1), (0, 0), (2, 2), (0, 1), (1, 0), (0, 2), (1, 1), (3, 2), (0, 3), (1, 2), (3, 3), (2, 3), (1, 3), )
SEND_START = (('wa', 3, 0), ('wa', 3, 1), ('wb', 3, 0), ('wb', 1, 0), )
SEND_BEFORE = (
    (),
    (),
    (('wf', 3, 0), ('wb', 2, 1), ),
    (('hd', 2), ),
    (('hd', 3), ('wa', 2, 1), ('wa', 2, 0), ('wf', 3, 1), ('wb', 0, 1), ),
    (),
    (('hd', 5), ('wa', 0, 1), ('hd', 4), ('wa', 0, 0), ),
    (),
    (('hd', 7), ('wb', 0, 0), ('wf', 2, 1), ('wb', 3, 1), ),
    (('wf', 2, 0), ),
    (),
    (),
    (('hd', 11), ('wb', 2, 0), ('hd', 8), ('hd', 10), ),
    (('hd', 12), ),
    (('hd', 13), ('wa', 1, 0), ),
    (('hd', 14), ),
)
SEND_AFTER = (
    (),
    (),
    (),
    (),
    (),
    (),
    (),
    (),
    (),
    (),
    (('hf', 7), ('hd', 1), ),
    (),
    (),
    (),
    (('hf', 11), ('wa', 1, 1), ),
    (),
)
SEND_END = (('hd', 15), ('wf', 0, 1), ('wf', 0, 0), ('wb', 1, 1), ('wf', 1, 0), ('lw', 2), ('lw', 3), )
SEND_MAKE = (
    (('hf', 14), ('hf', 15), ('hf', 8), ('hd', 0), ('hf', 10), ('wf', 1, 1), ('hd', 6), ('hd', 9), ),
    (),
    (),
    (),
    (('lw', 0), ),
    (),
    (),
    (('lw', 1), ),
    (),
    (('hf', 6), ),
    (),
    (),
    (),
    (),
    (),
    (),
)
SEND_JOIN = (
    (),
    (),
    (),
    (),
    (),
    (),
    (),
    (),
    (),
    (('hf', 9), ),
    (),
    (),
    (),
    (),
    (),
    (),
)
SEND_PRE = (
    (),
    (),
    (),
    (),
    (),
    (),
    (),
    (),
    (),
    (),
    (),
    (),
    (),
    (),
    (),
    (),
)


def order_of(i):
    last, r = i // 12, i % 3
    return (1 - last) * (r + r // 2) + 2 * last, (1 - last) * (i // 3) + last * (i - 12)


BATCH = {order_of(i): i for i in range(16)}
FIRST_STEP = {}
for place_in_order, (chunk_of, step_of) in enumerate(UNITS):
    FIRST_STEP.setdefault(step_of, place_in_order)
SENDS = [n for n, (_, j) in enumerate(UNITS) if j < 3]
FINALS = [n for n, (_, j) in enumerate(UNITS) if j == 3]


def place(y, q):
    high, low = y // 2, y % 2
    return 2 * ((high + q // 2) % 2) + (low + (q + 1) // 2) % 2


def look_up(table, n):
    value = jnp.int32(table[0])
    for at in range(1, len(table)):
        if table[at] != table[0]:
            value = jnp.where(n == at, table[at], value)
    return value


def routing_tables(ids, gates, experts, per_expert):
    rows = ids.shape[0]
    chosen = ids[:, :, None] == jnp.arange(experts, dtype=ids.dtype)
    picked = jnp.any(chosen, axis=1)
    weight = jnp.sum(jnp.where(chosen, gates[:, :, None], 0.0), axis=1)
    before = (jnp.arange(rows)[:, None] > jnp.arange(rows)[None, :]).astype(BF16)
    rank = jnp.dot(before, picked.astype(BF16), preferred_element_type=F32)
    rank = jnp.where(picked, rank, -1.0)
    hit = rank[:, :, None] == jnp.arange(per_expert, dtype=F32)
    row = jnp.arange(rows, dtype=F32)[:, None, None]
    position = jnp.sum(jnp.where(hit, row, 0.0), axis=0)
    value = jnp.sum(jnp.where(hit, weight[:, :, None], 0.0), axis=0)
    return position, value


def moe_kernel(nx, ny, x_ref, meta_ref, wg_ref, wu_ref, wd_ref, out_ref, tok_ref, h_ref, w_ref,
               metav, rb, db, ms, mr, ty_s, ty_r, tx_s, tx_r, td_s, td_r, hd_s, hd_r, hf_s, hf_r,
               wa_s, wa_r, wb_s, wb_r, wf_s, wf_r, rs_r, db_r, of_r, credit):
    rows, width = x_ref.shape
    half = rows // 2
    el, ff, _ = wg_ref.shape
    per = h_ref.shape[5]
    pairs = el * per
    kc, cw = w_ref.shape[0], w_ref.shape[4]
    ep_piece = el // PIECES
    eps = 2 * nx
    y = lax.axis_index('tp')
    ep = lax.axis_index('ep')
    x, c = ep // 2, ep % 2
    ya, yb, yo = place(y, A), place(y, B), place(y, O)
    yq = (y, ya, yb, yo)
    xp, xm = (x + 1) % nx, (x + nx - 1) % nx
    colb = ((y + y // 2) % 2) * (kc * cw)
    cola = ((ya + ya // 2) % 2) * (kc * cw)
    me = y * eps + ep

    dev_a = {'tp': ya, 'ep': ep}
    dev_b = {'tp': yb, 'ep': ep}
    dev_p = {'tp': y, 'ep': 2 * x + 1 - c}
    dev_xp = {'tp': y, 'ep': 2 * xp + c}
    dev_xm = {'tp': y, 'ep': 2 * xm + c}

    def remote(src, dst, send, recv, dev):
        return pltpu.make_async_remote_copy(src_ref=src, dst_ref=dst, send_sem=send, recv_sem=recv, device_id=dev, device_id_type=MESH)

    def lin(xs, ys, cs):
        return ys * eps + 2 * xs + cs

    def either(rel):
        return c if rel == 0 else 1 - c

    barrier = pltpu.get_barrier_semaphore()

    def peer_of(d):
        other = (me + d) % (ny * eps)
        return other // eps, other % eps

    def greet(d, carry):
        py, pe = peer_of(d)
        pl.semaphore_signal(barrier, inc=1, device_id={'tp': py, 'ep': pe}, device_id_type=MESH)
        return carry

    lax.fori_loop(1, ny * eps, greet, 0)
    pl.semaphore_wait(barrier, ny * eps - 1)

    def meta_copy(d):
        py, pe = peer_of(d)
        return remote(meta_ref.at[pe], metav.at[me], ms.at[d], mr.at[me], {'tp': py, 'ep': pe})

    def meta_send(d, carry):
        meta_copy(d).start()
        return carry

    lax.fori_loop(1, ny * eps, meta_send, 0)
    metav[me] = meta_ref[ep]

    def own(dxm, q):
        return tok_ref.at[(x + dxm) % nx, yq[q], c]

    def rows_of(ref, part):
        return ref.at[pl.ds(part * half, half)]

    def ty(n):
        if n < 2:
            return remote(x_ref, tok_ref.at[x, y, c], ty_s.at[n], ty_r.at[n], (dev_a, dev_b)[n])
        block = rows_of(own(0, (B, A)[n - 2]), n - 2)
        return remote(block, block, ty_s.at[n], ty_r.at[n], (dev_a, dev_b)[n - 2])

    def tx(q, n):
        if n < 2:
            return remote(x_ref if q == S else own(0, q), own(0, q), tx_s.at[q, n], tx_r.at[q, n], (dev_xp, dev_xm)[n])
        block = rows_of(own((3, 1)[n - 2], q), n - 2)
        return remote(block, block, tx_s.at[q, n], tx_r.at[q, n], (dev_xp, dev_xm)[n - 2])

    def td(q, dxm):
        return remote(x_ref if (q == S and dxm == 0) else own(dxm, q), own(dxm, q), td_s.at[q, dxm], td_r.at[q, dxm], dev_p)

    def wa(k, g):
        src = wd_ref.at[pl.ds(g * ep_piece, ep_piece), :, pl.ds(pl.multiple_of(cola + k * cw, cw), cw)]
        return remote(src, w_ref.at[k, y, pl.ds(g * ep_piece, ep_piece)], wa_s.at[k, g], wa_r.at[k, g], dev_a)

    def wb(k, g):
        src = wd_ref.at[pl.ds(g * ep_piece, ep_piece), :, pl.ds(pl.multiple_of(colb + k * cw, cw), cw)]
        return remote(src, w_ref.at[k, y, pl.ds(g * ep_piece, ep_piece)], wb_s.at[k, g], wb_r.at[k, g], dev_b)

    def wf(k, g):
        block = w_ref.at[k, ya, pl.ds(g * ep_piece, ep_piece)]
        return remote(block, block, wf_s.at[k, g], wf_r.at[k, g], dev_b)

    def hd(i):
        dxm, q = order_of(i)
        block = h_ref.at[y, (x + dxm) % nx, yq[q]]
        return remote(block, block, hd_s.at[i], hd_r.at[i], dev_a if q < 2 else dev_b)

    def hf(i):
        dxm, q = order_of(i)
        block = h_ref.at[yb, (x + dxm) % nx, place(yb, q)]
        return remote(block, block, hf_s.at[i], hf_r.at[i], dev_a)

    def send(actions, load_w=None):
        for action in actions:
            kind, at = action[0], action[1:]
            if kind == 'wf':
                wa(*at).wait_recv()
            if kind == 'hf':
                hd(*at).wait_recv()
            if kind == 'lw':
                load_w(*at)
            else:
                {'wa': wa, 'wb': wb, 'wf': wf, 'hd': hd, 'hf': hf}[kind](*at).start()

    for n in (0, 1):
        ty(n).start()
        tx(S, n).start()
    td(S, 0).start()
    send(SEND_START)

    def came(q):
        for n in (0, 1):
            tx(q, n).wait_recv()
        td(q, 1).start()
        td(q, 3).start()

    def both(q, first):
        tx(q, first).start()
        tx(q, first + 1).start()

    def comm(step):
        if step == 1:
            ty(0).wait_recv()
            ty(1).wait_recv()
            ty(2).start()
            ty(3).start()
            both(A, 0)
            both(B, 0)
            came(S)
            td(A, 0).start()
            td(B, 0).start()
        if step == 4:
            came(A)
            ty(2).wait_recv()
            ty(3).wait_recv()
            both(O, 0)
            both(S, 2)
            both(A, 2)
            td(O, 0).start()
        if step in (7, 10):
            q = {7: B, 10: O}[step]
            came(q)
            both(q, 2)
        if step >= 12:
            tx(step - 12, 2).wait_recv()
            tx(step - 12, 3).wait_recv()
            td(step - 12, 2).start()

    row_id = lax.broadcasted_iota(jnp.int32, (rows, pairs), 0)

    def one_hot(src):
        pos = metav[src, 0:1, :].astype(jnp.int32)
        return (row_id == pos).astype(F32).astype(BF16)

    def meta_wait(src):
        remote(meta_ref.at[0], metav.at[src], ms.at[0], mr.at[src], dev_p).wait_recv()

    def phase_one(wg, wu, tb, xg, hb, wl, tl, hl):
        load_g = pltpu.make_async_copy(wg_ref, wg, wl.at[0])
        load_u = pltpu.make_async_copy(wu_ref, wu, wl.at[1])
        load_g.start()
        load_u.start()

        def store(i):
            dxm, q = order_of(i)
            return pltpu.make_async_copy(hb, h_ref.at[y, (x + dxm) % nx, place(y, q)], hl.at[0])

        def batch(i, carry):
            @pl.when(i > 0)
            def _():
                store(i - 1).wait()

            for step in range(1, 16):
                if SEND_BEFORE[step] or SEND_AFTER[step] or step in (1, 4, 7, 10) or step >= 12:
                    @pl.when(i == step)
                    def _(step=step):
                        send(SEND_BEFORE[step])
                        comm(step)
                        send(SEND_AFTER[step])

            dxm, q = order_of(i)
            xs, ys = (x + dxm) % nx, place(y, q)
            mine = pltpu.make_async_copy(x_ref, tb.at[0], tl.at[0])
            other = pltpu.make_async_copy(tok_ref.at[xs, ys, c], tb.at[0], tl.at[0])
            theirs = pltpu.make_async_copy(tok_ref.at[xs, ys, 1 - c], tb.at[1], tl.at[1])

            @pl.when(i == 0)
            def _():
                mine.start()

            @pl.when(i > 0)
            def _():
                other.start()
                meta_wait(lin(xs, ys, c))

            remote(tok_ref.at[xs, ys, c], tok_ref.at[xs, ys, c], td_s.at[q, dxm], td_r.at[q, dxm], dev_p).wait_recv()
            theirs.start()
            meta_wait(lin(xs, ys, 1 - c))
            for s in (0, 1):
                (other, theirs)[s].wait()
                hot = one_hot(lin(xs, ys, either(s)))
                step = min(512, width)
                for lo in range(0, width, step):
                    got = lax.dot_general(hot, tb[s, :, lo:lo + step], (((0,), (0,)), ((), ())), preferred_element_type=F32)
                    xg[:, s, :, lo:lo + step] = got.astype(BF16).reshape(el, per, step)

            @pl.when(i == 0)
            def _():
                load_g.wait()
                load_u.wait()

            def expert(e, carry):
                lhs = xg[e].reshape(2 * per, width)
                a = lax.dot_general(lhs, wg[e], (((1,), (1,)), ((), ())), preferred_element_type=F32)
                b = lax.dot_general(lhs, wu[e], (((1,), (1,)), ((), ())), preferred_element_type=F32)
                hid = (a * jax.nn.sigmoid(a) * b).astype(BF16).reshape(2, per, ff)
                for s in (0, 1):
                    hb[either(s), e] = hid[s]
                return carry

            lax.fori_loop(0, el, expert, 0)
            store(i).start()
            return carry

        lax.fori_loop(0, 16, batch, 0)
        store(15).wait()

    pl.run_scoped(
        phase_one,
        pltpu.VMEM((el, ff, width), BF16),
        pltpu.VMEM((el, ff, width), BF16),
        pltpu.VMEM((2, rows, width), BF16),
        pltpu.VMEM((el, 2, per, width), BF16),
        pltpu.VMEM((2, el, per, ff), BF16),
        pltpu.SemaphoreType.DMA((2,)),
        pltpu.SemaphoreType.DMA((2,)),
        pltpu.SemaphoreType.DMA((1,)),
    )

    units = len(UNITS)

    def phase_two(wv, hv, gc, o3, pb, pp, sb, fb, wl, hvl, pp_s, rs_s, of_s, ol):
        lane = gc.shape[4]

        def blocks(j):
            return ((x + 2 * nx - 1 - j) % nx, (x + 1 + j) % nx), (y, ya)

        def w_loads(k):
            src = wd_ref.at[:, :, pl.ds(pl.multiple_of(colb + k * cw, cw), cw)]
            copies = [pltpu.make_async_copy(src, wv.at[k, S], wl.at[k, S])]
            for q in (A, B, O):
                copies.append(pltpu.make_async_copy(w_ref.at[k, yq[q]], wv.at[k, q], wl.at[k, q]))
            return copies

        def load_w(k):
            for g in range(PIECES):
                wb(k, g).wait_recv()
                wf(k, g).wait_recv()
            for copy in w_loads(k):
                copy.start()

        def h_loads(n, j):
            xs, ys = blocks(j)
            copies = []
            for d in (0, 1):
                for rel in (0, 1):
                    for q in (S, A, B, O):
                        copies.append(pltpu.make_async_copy(
                            h_ref.at[yq[q], xs[d], ys[d], either(rel)], hv.at[n % 2, q, :, 2 * d + rel], hvl.at[n % 2, q, 2 * d + rel]))
            return copies

        def first_use(j):
            minus, plus = (3 - j) % 4, (1 + j) % 4
            hd(BATCH[(minus, A)]).wait_recv()
            hd(BATCH[(plus, S)]).wait_recv()
            hf(BATCH[(minus, O)]).wait_recv()
            hf(BATCH[(plus, B)]).wait_recv()
            xs, ys = blocks(j)
            for d in (0, 1):
                for rel in (0, 1):
                    gate = metav[lin(xs[d], ys[d], either(rel)), 1:2, :]
                    gc[j, :, 2 * d + rel] = jnp.transpose(jnp.broadcast_to(gate, (lane, pairs))).reshape(el, per, lane)

        def partner_copy(n, d):
            return remote(pp.at[n % 2, d], db.at[n % 2, d], pp_s.at[n % 2, d], db_r.at[n % 2, d], dev_p)

        def ring_copy(slot, d, k, j):
            return remote(sb.at[slot, d], rb.at[d, k, j], rs_s.at[slot, d], rs_r.at[d, k, j], (dev_xp, dev_xm)[d])

        def out_copies(slot, k):
            cols = out_ref.at[:, pl.ds(pl.multiple_of(colb + k * cw, cw), cw)]
            return (
                pltpu.make_async_copy(fb.at[slot, 0], cols, ol.at[slot]),
                remote(fb.at[slot, 1], cols, of_s.at[slot], of_r.at[k], dev_a),
            )

        def make(n):
            k, j = look_up([u[0] for u in UNITS], n), look_up([u[1] for u in UNITS], n)
            xs, ys = blocks(j)
            for at in range(units):
                new_chunk = UNITS[at][0] not in [u[0] for u in UNITS[:at]]
                if (at and SEND_MAKE[at]) or new_chunk:
                    @pl.when(n == at)
                    def _(at=at, new_chunk=new_chunk):
                        if at:
                            send(SEND_MAKE[at], load_w)
                        if new_chunk:
                            for copy in w_loads(UNITS[at][0]):
                                copy.wait()
            for copy in h_loads(n, j):
                copy.wait()

            def expert(e, carry):
                o = jnp.zeros((4 * per, cw), F32)
                for q in (S, A, B, O):
                    o = o + jnp.dot(hv[n % 2, q, e].reshape(4 * per, ff), wv[k, q, e], preferred_element_type=F32)
                g = gc[j, e].reshape(4 * per, lane)
                v = o * jnp.concatenate([g] * (cw // lane), axis=1)
                hi = v.astype(BF16)
                rest = v - hi.astype(F32)
                mid = rest.astype(BF16)
                low = (rest - mid.astype(F32)).astype(BF16)
                o3[:, 0, e] = hi.reshape(4, per, cw)
                o3[:, 1, e] = mid.reshape(4, per, cw)
                o3[:, 2, e] = low.reshape(4, per, cw)
                return carry

            lax.fori_loop(0, el, expert, 0)

            @pl.when(n >= 2)
            def _():
                for d in (0, 1):
                    partner_copy(n - 2, d).wait_send()
                pl.semaphore_wait(credit, 1)

            for rel in (1, 0):
                for d in (0, 1):
                    hot = one_hot(lin(xs[d], ys[d], either(rel)))
                    total = jnp.dot(hot, o3[2 * d + rel, 0].reshape(pairs, cw), preferred_element_type=F32)
                    total += jnp.dot(hot, o3[2 * d + rel, 1].reshape(pairs, cw), preferred_element_type=F32)
                    total += jnp.dot(hot, o3[2 * d + rel, 2].reshape(pairs, cw), preferred_element_type=F32)
                    if rel == 1:
                        pp[n % 2, d] = total
                        partner_copy(n, d).start()
                    else:
                        pb[n % 2, d] = total

        def join(n):
            k, j = look_up([u[0] for u in UNITS], n), look_up([u[1] for u in UNITS], n)
            count = look_up([sum(1 for m in SENDS if m < at) for at in range(units)], n)
            slot = count % 4
            for at in range(units):
                if SEND_JOIN[at]:
                    @pl.when(n == at)
                    def _(at=at):
                        send(SEND_JOIN[at], load_w)
            for d in (0, 1):
                partner_copy(n, d).wait_recv()

            @pl.when((j < 3) & (count >= 4))
            def _():
                for d in (0, 1):
                    ring_copy(slot, d, k, 0).wait_send()

            for d in (0, 1):
                @pl.when(j == 0)
                def _():
                    sb[slot, d] = pb[n % 2, d] + db[n % 2, d]

                @pl.when((j > 0) & (j < 3))
                def _():
                    ring_copy(slot, d, k, j - 1).wait_recv()
                    sb[slot, d] = pb[n % 2, d] + db[n % 2, d] + rb[d, k, j - 1]

                @pl.when(j < 3)
                def _():
                    ring_copy(slot, d, k, j).start()

            for order, at in enumerate(FINALS):
                @pl.when(n == at)
                def _(order=order, at=at):
                    kk = UNITS[at][0]
                    if order >= 2:
                        local, away = out_copies(order % 2, kk)
                        local.wait()
                        away.wait_send()
                    for d in (0, 1):
                        ring_copy(0, d, kk, 2).wait_recv()
                        fb[order % 2, d] = (pb[at % 2, d] + db[at % 2, d] + rb[d, kk, 2]).astype(BF16)
                    local, away = out_copies(order % 2, kk)
                    local.start()
                    away.start()

            @pl.when(n < units - 2)
            def _():
                pl.semaphore_signal(credit, inc=1, device_id=dev_p, device_id_type=MESH)

        send([action for action in SEND_END if action[0] == 'lw'], load_w)
        send(SEND_MAKE[0], load_w)
        first_use(UNITS[0][1])
        for copy in h_loads(0, UNITS[0][1]):
            copy.start()
        seen = [int(at + 1 < units and FIRST_STEP[UNITS[at + 1][1]] <= at) for at in range(units)]

        def unit(n, carry):
            @pl.when(n < units)
            def _():
                make(n)

                @pl.when(look_up(seen, n) == 1)
                def _():
                    for copy in h_loads(n + 1, look_up([u[1] for u in UNITS[1:]], n)):
                        copy.start()

            @pl.when(n > 0)
            def _():
                join(n - 1)

            for step, at in FIRST_STEP.items():
                if at > 0:
                    @pl.when(n == at - 1)
                    def _(step=step, at=at):
                        send(SEND_PRE[at], load_w)
                        first_use(step)
                        for copy in h_loads(at, step):
                            copy.start()

            return carry

        lax.fori_loop(0, units + 1, unit, 0)
        for d in (0, 1):
            for n in (units - 2, units - 1):
                partner_copy(n, d).wait_send()
            for slot in range(4):
                ring_copy(slot, d, 0, 0).wait_send()
        for slot in (0, 1):
            local, away = out_copies(slot, 0)
            local.wait()
            away.wait_send()
        for k in range(kc):
            out_copies(0, k)[1].wait_recv()

    lane = min(128, cw)
    send([action for action in SEND_END if action[0] != 'lw'])

    pl.run_scoped(
        phase_two,
        pltpu.VMEM((kc, 4, el, ff, cw), BF16),
        pltpu.VMEM((2, 4, el, 4, per, ff), BF16),
        pltpu.VMEM((4, el, 4, per, lane), F32),
        pltpu.VMEM((4, 3, el, per, cw), BF16),
        pltpu.VMEM((2, 2, rows, cw), F32),
        pltpu.VMEM((2, 2, rows, cw), F32),
        pltpu.VMEM((4, 2, rows, cw), F32),
        pltpu.VMEM((2, 2, rows, cw), BF16),
        pltpu.SemaphoreType.DMA((kc, 4)),
        pltpu.SemaphoreType.DMA((2, 4, 4)),
        pltpu.SemaphoreType.DMA((2, 2)),
        pltpu.SemaphoreType.DMA((4, 2)),
        pltpu.SemaphoreType.DMA((2,)),
        pltpu.SemaphoreType.DMA((2,)),
    )

    def meta_done(d, carry):
        meta_copy(d).wait_send()
        return carry

    lax.fori_loop(1, ny * eps, meta_done, 0)
    for n in range(4):
        ty(n).wait_send()
    for q in (S, A, B, O):
        for n in range(4):
            tx(q, n).wait_send()
        for dxm in range(4):
            td(q, dxm).wait_send()
    for k in range(kc):
        for g in range(PIECES):
            wa(k, g).wait_send()
            wb(k, g).wait_send()
            wf(k, g).wait_send()
    for i in range(16):
        hd(i).wait_send()
        if order_of(i)[1] >= 2:
            hf(i).wait_send()


def solution(mesh):
    ny, eps = mesh.shape['tp'], mesh.shape['ep']
    nx = eps // 2
    row_spec = P(('dp', 'ep', 'tp'), None)
    w_in_spec = P('ep', None, 'tp')
    w_out_spec = P('ep', 'tp', None)

    def local_moe(x, ids, gates, w_gate, w_up, w_down):
        rows, width = x.shape
        el, _, ff = w_gate.shape
        experts = el * eps
        per = rows * ids.shape[1] // experts
        pairs = el * per
        cw = width // 2 // CHUNKS
        position, value = routing_tables(ids, gates, experts, per)
        meta = jnp.stack([position.reshape(eps, pairs), value.reshape(eps, pairs)], axis=1)
        meta = jnp.pad(meta, ((0, 0), (0, 6), (0, 0)))
        hbm = pl.BlockSpec(memory_space=pl.ANY)
        vmem = pl.BlockSpec(memory_space=pltpu.VMEM)
        dma = pltpu.SemaphoreType.DMA
        outs = pl.pallas_call(
            functools.partial(moe_kernel, nx, ny),
            name='moe_kernel',
            out_shape=[
                jax.ShapeDtypeStruct((rows, width), BF16),
                jax.ShapeDtypeStruct((nx, ny, 2, rows, width), BF16),
                jax.ShapeDtypeStruct((ny, nx, ny, 2, el, per, ff), BF16),
                jax.ShapeDtypeStruct((CHUNKS, ny, el, ff, cw), BF16),
            ],
            in_specs=[hbm, vmem, hbm, hbm, hbm],
            out_specs=[hbm] * 4,
            scratch_shapes=[
                pltpu.VMEM((ny * eps, 8, pairs), F32),
                pltpu.VMEM((2, CHUNKS, 3, rows, cw), F32),
                pltpu.VMEM((2, 2, rows, cw), F32),
                dma((ny * eps,)), dma((ny * eps,)),
                dma((4,)), dma((4,)),
                dma((4, 4)), dma((4, 4)),
                dma((4, 4)), dma((4, 4)),
                dma((16,)), dma((16,)), dma((16,)), dma((16,)),
            ] + [dma((CHUNKS, PIECES))] * 6 + [
                dma((2, CHUNKS, 3)), dma((2, 2)), dma((CHUNKS,)),
                pltpu.SemaphoreType.REGULAR,
            ],
            compiler_params=pltpu.CompilerParams(collective_id=0, has_side_effects=True, vmem_limit_bytes=67 * 1000 * 1000),
        )(x, meta, jnp.transpose(w_gate, (0, 2, 1)), jnp.transpose(w_up, (0, 2, 1)), w_down)
        return outs[0]

    return jax.shard_map(
        local_moe, mesh=mesh, in_specs=(row_spec, row_spec, row_spec, w_in_spec, w_in_spec, w_out_spec),
        out_specs=row_spec, check_vma=False)
```

time: 663 us -> 518 us (0.78)
  Pallas kernels: 622 us -> 509 us
  local copies, waits for them, and re-layouts: 35 us -> 3.35 us
    pallas_call x1, Pallas kernels: 622 us -> 509 us  [local_moe(): pl.pallas_call(functools.partial(moe_kernel, nx, ny), name='moe_kernel',...]
    unnamed x3 -> x1, local copies, waits for them, and re-layouts: 34.8 us -> 3.16 us
where the time goes in v2:
time: 518 us; the launch traced here: 516 us
  Pallas kernels  509 us (98%)
    pallas_call x1, Pallas kernels, local_moe(): pl.pallas_call(functools.partial(moe_kernel, nx, ny), name='moe_kernel',...  509 us

profile of v2, /device:TPU:97, one launch (start us, length us, event | category | flops | bytes accessed | tf_op | source)
XLA Modules:
  0.0 516.4 jit_solution(9868210121031008199)
XLA Ops:
  0.0 0.8 fusion
  0.8 0.3 convolution_select_fusion
  1.1 0.8 select_reduce_fusion.2
  1.9 1.3 select_reduce_fusion.1
  3.3 0.1 stack_reshape.8
  3.3 0.1 stack_reshape.9
  3.4 0.7 select_maximum_fusion.meta_ref
  4.1 509.1 %moe_kernel.1 = (bf16[512,2048]{1,0:T(8,128)(2,1)}, bf16[4,4,2,512,2048]{4,3,2,1,0:T(8,128)(2,1)}, bf16[4,4,4,2,8,48,352]{6,5,4,3,2,1,0:T(8,128)(2,1)}, bf16[4,4,8,352,256]{4,3,2,1,0:T(8,128)(2,1)}) custom-call(bf16[512,2048]{1,0:T(8,128)(2,1)} %x_ref.1, f32[8,8,384]{2,1,0:T(8,128)} %select_maximum_fusion.meta_ref, bf16[8,352,2048]{2,1,0:T(8,128)(2,1)} %bitcast.3, ...), custom_call_target="tpu_custom_call" | custom-call | tf_op jit(solution)/shard_map/moe_kernel/pallas_call | solution.py:672
  513.2 3.2 copy.18

commit v3 on v2

--- a/solution.py
+++ b/solution.py
@@ -9,31 +9,35 @@
 
 MESH = pl.DeviceIdType.MESH
 CHUNKS = 4
+LANES = 256
 PIECES = 2
 BF16 = jnp.bfloat16
 F32 = jnp.float32
 
 S, A, B, O = 0, 1, 2, 3
 
-UNITS = ((3, 0), (2, 0), (2, 1), (3, 1), (0, 0), (2, 2), (0, 1), (1, 0), (0, 2), (1, 1), (3, 2), (0, 3), (1, 2), (3, 3), (2, 3), (1, 3), )
-SEND_START = (('wa', 3, 0), ('wa', 3, 1), ('wb', 3, 0), ('wb', 1, 0), )
+UNITS = ((2, 0), (1, 0), (0, 0), (2, 1), (0, 1), (1, 1), (0, 2), (3, 0), (1, 2), (3, 1), (2, 2), (1, 3), (3, 2), (0, 3), (2, 3), (3, 3), )
+ORDER = ((0, 0), (0, 1), (1, 0), (0, 2), (1, 1), (1, 2), (0, 3), (0, 4), (1, 3), (1, 4), (0, 5), (0, 6), (1, 5), (1, 6), (0, 7), (0, 8), (1, 7), (0, 9), (1, 8), (0, 10), (1, 9), (1, 10), (0, 11), (0, 12), (1, 11), (0, 13), (1, 12), (0, 14), (1, 13), (0, 15), (1, 14), (1, 15), )
+OPPOSITE_VIA_A = 4
+OPPOSITE = (2,)
+SEND_START = (('wa', 1, 1), ('wb', 3, 1), ('wb', 1, 0), )
 SEND_BEFORE = (
     (),
     (),
-    (('wf', 3, 0), ('wb', 2, 1), ),
-    (('hd', 2), ),
-    (('hd', 3), ('wa', 2, 1), ('wa', 2, 0), ('wf', 3, 1), ('wb', 0, 1), ),
-    (),
-    (('hd', 5), ('wa', 0, 1), ('hd', 4), ('wa', 0, 0), ),
-    (),
-    (('hd', 7), ('wb', 0, 0), ('wf', 2, 1), ('wb', 3, 1), ),
+    (('hd', 1), ('wa', 2, 0), ('wa', 0, 1), ('wa', 2, 1), ('wa', 3, 0), ('wa', 1, 0), ('wa', 0, 0), ('wf', 1, 1), ('wb', 2, 0), ('wb', 0, 0), ('wb', 0, 1), ('wb', 1, 1), ('wb', 2, 1), ),
+    (),
+    (),
+    (),
+    (),
     (('wf', 2, 0), ),
     (),
-    (),
-    (('hd', 11), ('wb', 2, 0), ('hd', 8), ('hd', 10), ),
-    (('hd', 12), ),
-    (('hd', 13), ('wa', 1, 0), ),
-    (('hd', 14), ),
+    (('hd', 8), ('hd', 7), ('wf', 0, 1), ),
+    (),
+    (('hf', 8), ('wa', 3, 1), ('hd', 5), ('wf', 1, 0), ),
+    (('hd', 11), ('hd', 10), ('wf', 0, 0), ('wf', 2, 1), ),
+    (('hd', 12), ('hf', 7), ),
+    (('hf', 11), ('hd', 13), ),
+    (('hf', 10), ('hd', 14), ),
 )
 SEND_AFTER = (
     (),
@@ -46,25 +50,25 @@
     (),
     (),
     (),
-    (('hf', 7), ('hd', 1), ),
-    (),
-    (),
-    (),
-    (('hf', 11), ('wa', 1, 1), ),
+    (),
+    (),
+    (),
+    (),
+    (),
     (),
 )
-SEND_END = (('hd', 15), ('wf', 0, 1), ('wf', 0, 0), ('wb', 1, 1), ('wf', 1, 0), ('lw', 2), ('lw', 3), )
+SEND_END = (('hd', 15), ('wf', 3, 1), ('hd', 9), ('wf', 3, 0), ('wb', 3, 0), ('hd', 6), ('lw', 0), ('lw', 1), ('lw', 2), )
 SEND_MAKE = (
-    (('hf', 14), ('hf', 15), ('hf', 8), ('hd', 0), ('hf', 10), ('wf', 1, 1), ('hd', 6), ('hd', 9), ),
-    (),
-    (),
-    (),
-    (('lw', 0), ),
-    (),
-    (),
-    (('lw', 1), ),
-    (),
-    (('hf', 6), ),
+    (),
+    (('hf', 14), ),
+    (),
+    (),
+    (),
+    (),
+    (),
+    (('lw', 3), ),
+    (),
+    (),
     (),
     (),
     (),
@@ -74,31 +78,13 @@
 )
 SEND_JOIN = (
     (),
-    (),
-    (),
-    (),
-    (),
-    (),
-    (),
-    (),
+    (('hf', 15), ('hd', 2), ('hd', 4), ('hd', 0), ('hd', 3), ),
     (),
     (('hf', 9), ),
     (),
     (),
     (),
-    (),
-    (),
-    (),
-)
-SEND_PRE = (
-    (),
-    (),
-    (),
-    (),
-    (),
-    (),
-    (),
-    (),
+    (('hf', 6), ),
     (),
     (),
     (),
@@ -158,6 +144,9 @@
     half = rows // 2
     el, ff, _ = wg_ref.shape
     per = h_ref.shape[5]
+    rest = ff - LANES * (ff // LANES)
+    whole = el * (ff // LANES)
+    assert ff // LANES == 1 and (el * rest) % LANES == 0 and rest <= 128
     pairs = el * per
     kc, cw = w_ref.shape[0], w_ref.shape[4]
     ep_piece = el // PIECES
@@ -215,13 +204,14 @@
     def own(dxm, q):
         return tok_ref.at[(x + dxm) % nx, yq[q], c]
 
-    def rows_of(ref, part):
-        return ref.at[pl.ds(part * half, half)]
+    def rows_of(ref, part, cut=None):
+        cut = half if cut is None else cut
+        return ref.at[pl.ds(part * cut, (cut, rows - cut)[part])]
 
     def ty(n):
         if n < 2:
             return remote(x_ref, tok_ref.at[x, y, c], ty_s.at[n], ty_r.at[n], (dev_a, dev_b)[n])
-        block = rows_of(own(0, (B, A)[n - 2]), n - 2)
+        block = rows_of(own(0, (B, A)[n - 2]), n - 2, rows * OPPOSITE_VIA_A // 4)
         return remote(block, block, ty_s.at[n], ty_r.at[n], (dev_a, dev_b)[n - 2])
 
     def tx(q, n):
@@ -287,8 +277,8 @@
         if step == 1:
             ty(0).wait_recv()
             ty(1).wait_recv()
-            ty(2).start()
-            ty(3).start()
+            for n in OPPOSITE:
+                ty(n).start()
             both(A, 0)
             both(B, 0)
             came(S)
@@ -296,8 +286,8 @@
             td(B, 0).start()
         if step == 4:
             came(A)
-            ty(2).wait_recv()
-            ty(3).wait_recv()
+            for n in OPPOSITE:
+                ty(n).wait_recv()
             both(O, 0)
             both(S, 2)
             both(A, 2)
@@ -320,7 +310,7 @@
     def meta_wait(src):
         remote(meta_ref.at[0], metav.at[src], ms.at[0], mr.at[src], dev_p).wait_recv()
 
-    def phase_one(wg, wu, tb, xg, hb, wl, tl, hl):
+    def phase_one(wg, wu, tb, xg, hb, left, wl, tl, hl):
         load_g = pltpu.make_async_copy(wg_ref, wg, wl.at[0])
         load_u = pltpu.make_async_copy(wu_ref, wu, wl.at[1])
         load_g.start()
@@ -374,16 +364,18 @@
                 load_g.wait()
                 load_u.wait()
 
-            def expert(e, carry):
+            for e in range(el):
                 lhs = xg[e].reshape(2 * per, width)
                 a = lax.dot_general(lhs, wg[e], (((1,), (1,)), ((), ())), preferred_element_type=F32)
                 b = lax.dot_general(lhs, wu[e], (((1,), (1,)), ((), ())), preferred_element_type=F32)
-                hid = (a * jax.nn.sigmoid(a) * b).astype(BF16).reshape(2, per, ff)
+                hid = a * jax.nn.sigmoid(a) * b
                 for s in (0, 1):
-                    hb[either(s), e] = hid[s]
-                return carry
-
-            lax.fori_loop(0, el, expert, 0)
+                    hb[either(s), e] = hid[s * per:(s + 1) * per, :LANES].astype(BF16)
+                left[e] = hid[:, LANES:]
+            packed = jnp.concatenate([left[e] for e in range(el)], axis=1).astype(BF16)
+            for m in range(el * rest // LANES):
+                for s in (0, 1):
+                    hb[either(s), whole + m] = packed[s * per:(s + 1) * per, m * LANES:(m + 1) * LANES]
             store(i).start()
             return carry
 
@@ -396,25 +388,49 @@
         pltpu.VMEM((el, ff, width), BF16),
         pltpu.VMEM((2, rows, width), BF16),
         pltpu.VMEM((el, 2, per, width), BF16),
-        pltpu.VMEM((2, el, per, ff), BF16),
+        pltpu.VMEM((2,) + h_ref.shape[4:], BF16),
+        pltpu.VMEM((el, 2 * per, rest), F32),
         pltpu.SemaphoreType.DMA((2,)),
         pltpu.SemaphoreType.DMA((2,)),
         pltpu.SemaphoreType.DMA((1,)),
     )
 
+    def window(e):
+        return e * rest // 128 * 128, -(-(e + 1) * rest // 128) * 128
+
+    def offset(e, q):
+        before = sum(LANES + window(m)[1] - window(m)[0] for m in range(e))
+        return 4 * before + q * (LANES + window(e)[1] - window(e)[0])
+
+    deep = offset(el, S)
+
     units = len(UNITS)
 
     def phase_two(wv, hv, gc, o3, pb, pp, sb, fb, wl, hvl, pp_s, rs_s, of_s, ol):
-        lane = gc.shape[4]
+        lane = gc.shape[3]
+
+        def clear(i, carry):
+            wv[i // 8, pl.ds(pl.multiple_of(i % 8 * (deep // 8), 16), deep // 8)] = jnp.zeros((deep // 8, cw), BF16)
+            return carry
+
+        lax.fori_loop(0, 8 * kc, clear, 0)
 
         def blocks(j):
             return ((x + 2 * nx - 1 - j) % nx, (x + 1 + j) % nx), (y, ya)
 
         def w_loads(k):
-            src = wd_ref.at[:, :, pl.ds(pl.multiple_of(colb + k * cw, cw), cw)]
-            copies = [pltpu.make_async_copy(src, wv.at[k, S], wl.at[k, S])]
-            for q in (A, B, O):
-                copies.append(pltpu.make_async_copy(w_ref.at[k, yq[q]], wv.at[k, q], wl.at[k, q]))
+            copies = []
+            for q in (S, A, B, O):
+                for e in range(el):
+                    if q == S:
+                        src = wd_ref.at[e, :, pl.ds(pl.multiple_of(colb + k * cw, cw), cw)]
+                    else:
+                        src = w_ref.at[k, yq[q], e]
+                    low, high = window(e)
+                    at = offset(e, q)
+                    copies.append(pltpu.make_async_copy(src.at[pl.ds(0, LANES)], wv.at[k, pl.ds(at, LANES)], wl.at[k]))
+                    copies.append(pltpu.make_async_copy(
+                        src.at[pl.ds(LANES, rest)], wv.at[k, pl.ds(at + LANES + e * rest - low, rest)], wl.at[k]))
             return copies
 
         def load_w(k):
@@ -440,11 +456,6 @@
             hd(BATCH[(plus, S)]).wait_recv()
             hf(BATCH[(minus, O)]).wait_recv()
             hf(BATCH[(plus, B)]).wait_recv()
-            xs, ys = blocks(j)
-            for d in (0, 1):
-                for rel in (0, 1):
-                    gate = metav[lin(xs[d], ys[d], either(rel)), 1:2, :]
-                    gc[j, :, 2 * d + rel] = jnp.transpose(jnp.broadcast_to(gate, (lane, pairs))).reshape(el, per, lane)
 
         def partner_copy(n, d):
             return remote(pp.at[n % 2, d], db.at[n % 2, d], pp_s.at[n % 2, d], db_r.at[n % 2, d], dev_p)
@@ -464,33 +475,39 @@
             xs, ys = blocks(j)
             for at in range(units):
                 new_chunk = UNITS[at][0] not in [u[0] for u in UNITS[:at]]
-                if (at and SEND_MAKE[at]) or new_chunk:
+                first = at in FIRST_STEP.values()
+                if (not first and SEND_MAKE[at]) or new_chunk:
                     @pl.when(n == at)
-                    def _(at=at, new_chunk=new_chunk):
-                        if at:
+                    def _(at=at, new_chunk=new_chunk, first=first):
+                        if not first:
                             send(SEND_MAKE[at], load_w)
                         if new_chunk:
-                            for copy in w_loads(UNITS[at][0]):
-                                copy.wait()
+                            pltpu.make_async_copy(w_ref.at[UNITS[at][0]], w_ref.at[UNITS[at][0]], wl.at[UNITS[at][0]]).wait()
+            for d in (0, 1):
+                for rel in (0, 1):
+                    gate = metav[lin(xs[d], ys[d], either(rel)), 1:2, :]
+                    gc[:, 2 * d + rel] = jnp.transpose(jnp.broadcast_to(gate, (lane, pairs))).reshape(el, per, lane)
             for copy in h_loads(n, j):
                 copy.wait()
 
-            def expert(e, carry):
-                o = jnp.zeros((4 * per, cw), F32)
+            for e in range(el):
+                low, high = window(e)
+                parts = []
                 for q in (S, A, B, O):
-                    o = o + jnp.dot(hv[n % 2, q, e].reshape(4 * per, ff), wv[k, q, e], preferred_element_type=F32)
-                g = gc[j, e].reshape(4 * per, lane)
+                    parts.append(hv[n % 2, q, e].reshape(4 * per, LANES))
+                    for at in range(low, high, 128):
+                        parts.append(hv[n % 2, q, whole + at // LANES, :, :, at % LANES:at % LANES + 128].reshape(4 * per, 128))
+                size = 4 * (LANES + high - low)
+                o = jnp.dot(jnp.concatenate(parts, axis=1), wv[k, offset(e, S):offset(e, S) + size], preferred_element_type=F32)
+                g = gc[e].reshape(4 * per, lane)
                 v = o * jnp.concatenate([g] * (cw // lane), axis=1)
                 hi = v.astype(BF16)
-                rest = v - hi.astype(F32)
-                mid = rest.astype(BF16)
-                low = (rest - mid.astype(F32)).astype(BF16)
+                over = v - hi.astype(F32)
+                mid = over.astype(BF16)
+                low_part = (over - mid.astype(F32)).astype(BF16)
                 o3[:, 0, e] = hi.reshape(4, per, cw)
                 o3[:, 1, e] = mid.reshape(4, per, cw)
-                o3[:, 2, e] = low.reshape(4, per, cw)
-                return carry
-
-            lax.fori_loop(0, el, expert, 0)
+                o3[:, 2, e] = low_part.reshape(4, per, cw)
 
             @pl.when(n >= 2)
             def _():
@@ -567,9 +584,20 @@
             copy.start()
         seen = [int(at + 1 < units and FIRST_STEP[UNITS[at + 1][1]] <= at) for at in range(units)]
 
-        def unit(n, carry):
-            @pl.when(n < units)
-            def _():
+        def operation(at, carry):
+            n = look_up([o[1] for o in ORDER], at)
+
+            @pl.when(look_up([o[0] for o in ORDER], at) == 0)
+            def _():
+                for step, first in FIRST_STEP.items():
+                    if first > 0:
+                        @pl.when(n == first)
+                        def _(step=step, first=first):
+                            send(SEND_MAKE[first], load_w)
+                            first_use(step)
+                            for copy in h_loads(first, step):
+                                copy.start()
+
                 make(n)
 
                 @pl.when(look_up(seen, n) == 1)
@@ -577,22 +605,13 @@
                     for copy in h_loads(n + 1, look_up([u[1] for u in UNITS[1:]], n)):
                         copy.start()
 
-            @pl.when(n > 0)
-            def _():
-                join(n - 1)
-
-            for step, at in FIRST_STEP.items():
-                if at > 0:
-                    @pl.when(n == at - 1)
-                    def _(step=step, at=at):
-                        send(SEND_PRE[at], load_w)
-                        first_use(step)
-                        for copy in h_loads(at, step):
-                            copy.start()
+            @pl.when(look_up([o[0] for o in ORDER], at) == 1)
+            def _():
+                join(n)
 
             return carry
 
-        lax.fori_loop(0, units + 1, unit, 0)
+        lax.fori_loop(0, len(ORDER), operation, 0)
         for d in (0, 1):
             for n in (units - 2, units - 1):
                 partner_copy(n, d).wait_send()
@@ -610,15 +629,15 @@
 
     pl.run_scoped(
         phase_two,
-        pltpu.VMEM((kc, 4, el, ff, cw), BF16),
-        pltpu.VMEM((2, 4, el, 4, per, ff), BF16),
-        pltpu.VMEM((4, el, 4, per, lane), F32),
+        pltpu.VMEM((kc, deep, cw), BF16),
+        pltpu.VMEM((2, 4, h_ref.shape[4], 4, per, LANES), BF16),
+        pltpu.VMEM((el, 4, per, lane), F32),
         pltpu.VMEM((4, 3, el, per, cw), BF16),
         pltpu.VMEM((2, 2, rows, cw), F32),
         pltpu.VMEM((2, 2, rows, cw), F32),
         pltpu.VMEM((4, 2, rows, cw), F32),
         pltpu.VMEM((2, 2, rows, cw), BF16),
-        pltpu.SemaphoreType.DMA((kc, 4)),
+        pltpu.SemaphoreType.DMA((kc,)),
         pltpu.SemaphoreType.DMA((2, 4, 4)),
         pltpu.SemaphoreType.DMA((2, 2)),
         pltpu.SemaphoreType.DMA((4, 2)),
@@ -631,7 +650,7 @@
         return carry
 
     lax.fori_loop(1, ny * eps, meta_done, 0)
-    for n in range(4):
+    for n in (0, 1) + OPPOSITE:
         ty(n).wait_send()
     for q in (S, A, B, O):
         for n in range(4):
@@ -675,7 +694,7 @@
             out_shape=[
                 jax.ShapeDtypeStruct((rows, width), BF16),
                 jax.ShapeDtypeStruct((nx, ny, 2, rows, width), BF16),
-                jax.ShapeDtypeStruct((ny, nx, ny, 2, el, per, ff), BF16),
+                jax.ShapeDtypeStruct((ny, nx, ny, 2, el * ff // LANES, per, LANES), BF16),
                 jax.ShapeDtypeStruct((CHUNKS, ny, el, ff, cw), BF16),
             ],
             in_specs=[hbm, vmem, hbm, hbm, hbm],

time: 518 us -> 478 us (0.923)
  Pallas kernels: 509 us -> 470 us
    pallas_call x1, Pallas kernels: 509 us -> 470 us  [local_moe(): pl.pallas_call(functools.partial(moe_kernel, nx, ny), name='moe_kernel',...]
where the time goes in v3:
time: 478 us
  Pallas kernels  470 us (98%)
    pallas_call x1, Pallas kernels, local_moe(): pl.pallas_call(functools.partial(moe_kernel, nx, ny), name='moe_kernel',...  470 us

profile of v3, /device:TPU:97, one launch (start us, length us, event | category | flops | bytes accessed | tf_op | source)
XLA Modules:
  0.0 477.5 jit_solution(4449142414766823360)
XLA Ops:
  0.0 0.8 fusion
  0.8 0.3 convolution_select_fusion
  1.1 0.8 select_reduce_fusion.2
  1.9 1.3 select_reduce_fusion.1
  3.3 0.1 stack_reshape.8
  3.3 0.1 stack_reshape.9
  3.4 0.7 select_maximum_fusion.meta_ref
  4.1 470.3 %moe_kernel.1 = (bf16[512,2048]{1,0:T(8,128)(2,1)}, bf16[4,4,2,512,2048]{4,3,2,1,0:T(8,128)(2,1)}, bf16[4,4,4,2,11,48,256]{6,5,4,3,2,1,0:T(8,128)(2,1)}, bf16[4,4,8,352,256]{4,3,2,1,0:T(8,128)(2,1)}) custom-call(bf16[512,2048]{1,0:T(8,128)(2,1)} %x_ref.1, f32[8,8,384]{2,1,0:T(8,128)} %select_maximum_fusion.meta_ref, bf16[8,352,2048]{2,1,0:T(8,128)(2,1)} %bitcast.3, ...), custom_call_target="tpu_custom_call" | custom-call | tf_op jit(solution)/shard_map/moe_kernel/pallas_call | solution.py:691
  474.4 3.2 copy.18

commit v4 on v3

--- a/solution.py
+++ b/solution.py
@@ -16,28 +16,28 @@
 
 S, A, B, O = 0, 1, 2, 3
 
-UNITS = ((2, 0), (1, 0), (0, 0), (2, 1), (0, 1), (1, 1), (0, 2), (3, 0), (1, 2), (3, 1), (2, 2), (1, 3), (3, 2), (0, 3), (2, 3), (3, 3), )
-ORDER = ((0, 0), (0, 1), (1, 0), (0, 2), (1, 1), (1, 2), (0, 3), (0, 4), (1, 3), (1, 4), (0, 5), (0, 6), (1, 5), (1, 6), (0, 7), (0, 8), (1, 7), (0, 9), (1, 8), (0, 10), (1, 9), (1, 10), (0, 11), (0, 12), (1, 11), (0, 13), (1, 12), (0, 14), (1, 13), (0, 15), (1, 14), (1, 15), )
-OPPOSITE_VIA_A = 4
-OPPOSITE = (2,)
-SEND_START = (('wa', 1, 1), ('wb', 3, 1), ('wb', 1, 0), )
+UNITS = ((1, 0), (2, 0), (0, 0), (1, 1), (0, 1), (2, 1), (1, 2), (3, 0), (2, 2), (3, 1), (0, 2), (1, 3), (3, 2), (2, 3), (0, 3), (3, 3), )
+ORDER = ((0, 0), (0, 1), (1, 0), (0, 2), (1, 1), (1, 2), (0, 3), (0, 4), (1, 3), (0, 5), (1, 4), (0, 6), (1, 5), (1, 6), (0, 7), (0, 8), (1, 7), (0, 9), (1, 8), (0, 10), (1, 9), (0, 11), (1, 10), (0, 12), (1, 11), (0, 13), (1, 12), (0, 14), (1, 13), (0, 15), (1, 14), (1, 15), )
+OPPOSITE_VIA_A = 3
+OPPOSITE = (2, 3)
+SEND_START = (('wa', 1, 0), ('wb', 2, 1), ('wb', 0, 1), ('wb', 2, 0), )
 SEND_BEFORE = (
     (),
     (),
-    (('hd', 1), ('wa', 2, 0), ('wa', 0, 1), ('wa', 2, 1), ('wa', 3, 0), ('wa', 1, 0), ('wa', 0, 0), ('wf', 1, 1), ('wb', 2, 0), ('wb', 0, 0), ('wb', 0, 1), ('wb', 1, 1), ('wb', 2, 1), ),
-    (),
-    (),
-    (),
-    (),
-    (('wf', 2, 0), ),
-    (),
-    (('hd', 8), ('hd', 7), ('wf', 0, 1), ),
-    (),
-    (('hf', 8), ('wa', 3, 1), ('hd', 5), ('wf', 1, 0), ),
-    (('hd', 11), ('hd', 10), ('wf', 0, 0), ('wf', 2, 1), ),
-    (('hd', 12), ('hf', 7), ),
-    (('hf', 11), ('hd', 13), ),
-    (('hf', 10), ('hd', 14), ),
+    (('hd', 1, 1), ('wf', 1, 0), ('wb', 1, 0), ('wb', 1, 1), ),
+    (('hd', 2, 0), ('wa', 0, 1), ('wa', 2, 1), ('wa', 2, 0), ('wa', 0, 0), ('wa', 1, 1), ('wa', 3, 0), ('wa', 3, 1), ),
+    (),
+    (),
+    (('hd', 5, 1), ('hd', 1, 0), ('wf', 0, 1), ),
+    (),
+    (('hd', 7, 0), ('hd', 7, 1), ),
+    (('hd', 8, 0), ('hd', 8, 1), ('wf', 2, 1), ('wf', 2, 0), ),
+    (),
+    (('hf', 8, 1), ('hf', 7, 1), ('hd', 5, 0), ('hf', 7, 0), ('hf', 8, 0), ('hd', 10, 1), ('hd', 10, 0), ),
+    (('hd', 11, 0), ('hd', 11, 1), ('wf', 0, 0), ('wf', 1, 1), ('wb', 0, 0), ),
+    (),
+    (('hf', 11, 0), ('hd', 12, 0), ('hf', 10, 0), ('hf', 11, 1), ('hd', 13, 1), ('hd', 12, 1), ('hd', 13, 0), ('hf', 10, 1), ),
+    (('hd', 14, 0), ('hd', 14, 1), ),
 )
 SEND_AFTER = (
     (),
@@ -57,17 +57,17 @@
     (),
     (),
 )
-SEND_END = (('hd', 15), ('wf', 3, 1), ('hd', 9), ('wf', 3, 0), ('wb', 3, 0), ('hd', 6), ('lw', 0), ('lw', 1), ('lw', 2), )
+SEND_END = (('hf', 14, 0), ('hd', 15, 1), ('hd', 15, 0), ('wf', 3, 1), ('wf', 3, 0), ('wb', 3, 1), ('wb', 3, 0), ('hd', 6, 0), ('hd', 9, 1), ('hd', 6, 1), ('hd', 9, 0), ('lw', 0), ('lw', 1), ('lw', 2), )
 SEND_MAKE = (
     (),
-    (('hf', 14), ),
+    (('hf', 14, 1), ),
     (),
     (),
     (),
     (),
     (),
     (('lw', 3), ),
-    (),
+    (('hf', 6, 0), ),
     (),
     (),
     (),
@@ -77,16 +77,16 @@
     (),
 )
 SEND_JOIN = (
-    (),
-    (('hf', 15), ('hd', 2), ('hd', 4), ('hd', 0), ('hd', 3), ),
-    (),
-    (('hf', 9), ),
-    (),
-    (),
-    (),
-    (('hf', 6), ),
-    (),
-    (),
+    (('hf', 15, 1), ),
+    (('hf', 15, 0), ('hd', 4, 0), ('hd', 2, 1), ('hd', 3, 0), ('hd', 0, 0), ('hd', 4, 1), ('hd', 0, 1), ('hd', 3, 1), ),
+    (),
+    (),
+    (),
+    (),
+    (),
+    (('hf', 9, 1), ),
+    (('hf', 6, 1), ),
+    (('hf', 9, 0), ),
     (),
     (),
     (),
@@ -122,23 +122,57 @@
     return value
 
 
-def routing_tables(ids, gates, experts, per_expert):
-    rows = ids.shape[0]
-    chosen = ids[:, :, None] == jnp.arange(experts, dtype=ids.dtype)
-    picked = jnp.any(chosen, axis=1)
-    weight = jnp.sum(jnp.where(chosen, gates[:, :, None], 0.0), axis=1)
-    before = (jnp.arange(rows)[:, None] > jnp.arange(rows)[None, :]).astype(BF16)
-    rank = jnp.dot(before, picked.astype(BF16), preferred_element_type=F32)
-    rank = jnp.where(picked, rank, -1.0)
-    hit = rank[:, :, None] == jnp.arange(per_expert, dtype=F32)
-    row = jnp.arange(rows, dtype=F32)[:, None, None]
-    position = jnp.sum(jnp.where(hit, row, 0.0), axis=0)
-    value = jnp.sum(jnp.where(hit, weight[:, :, None], 0.0), axis=0)
-    return position, value
-
-
-def moe_kernel(nx, ny, x_ref, meta_ref, wg_ref, wu_ref, wd_ref, out_ref, tok_ref, h_ref, w_ref,
-               metav, rb, db, ms, mr, ty_s, ty_r, tx_s, tx_r, td_s, td_r, hd_s, hd_r, hf_s, hf_r,
+def routing_tables(ids_ref, gate_ref, meta_ref, slot_ref, weight_ref, per):
+    top, rows = ids_ref.shape
+    experts = slot_ref.shape[0]
+    devices, _, pairs = meta_ref.shape
+    group = experts // devices
+    expert = lax.broadcasted_iota(jnp.int32, (experts, rows), 0)
+    chosen = jnp.zeros((experts, rows), F32)
+    weight = jnp.zeros((experts, rows), F32)
+    for j in range(top):
+        here = expert == ids_ref[j:j + 1, :]
+        chosen = jnp.where(here, 1.0, chosen)
+        weight = jnp.where(here, gate_ref[j:j + 1, :], weight)
+    earlier = lax.broadcasted_iota(jnp.int32, (rows, rows), 0) < lax.broadcasted_iota(jnp.int32, (rows, rows), 1)
+    rank = jnp.dot(chosen.astype(BF16), earlier.astype(F32).astype(BF16), preferred_element_type=F32)
+    slot_ref[...] = jnp.where(chosen > 0.0, rank, -1.0)
+    weight_ref[...] = weight
+    lane = lax.broadcasted_iota(jnp.int32, (group, pairs), 1)
+    sub = lax.broadcasted_iota(jnp.int32, (group, pairs), 0)
+    mine = ((lane >= sub * per) & (lane < (sub + 1) * per)).astype(F32).astype(BF16)
+    place_in_expert = lax.broadcasted_iota(jnp.int32, (rows, pairs), 1)
+    for m in range(1, group):
+        place_in_expert = jnp.where(lax.broadcasted_iota(jnp.int32, (rows, pairs), 1) >= m * per,
+                                    lax.broadcasted_iota(jnp.int32, (rows, pairs), 1) - m * per, place_in_expert)
+    place_in_expert = place_in_expert.astype(F32)
+    row = lax.broadcasted_iota(jnp.int32, (8, rows), 1)
+    high = (row // 2).astype(F32).astype(BF16)
+    low = (row % 2).astype(F32).astype(BF16)
+    top_row = lax.broadcasted_iota(jnp.int32, (8, pairs), 0)
+
+    def spread(part):
+        return lax.dot_general(part, mine, (((0,), (0,)), ((), ())), preferred_element_type=F32)
+
+    def table(d, carry):
+        at = pl.ds(pl.multiple_of(d * group, group), group)
+        hit = (spread(slot_ref[at, :].astype(BF16)) == place_in_expert).astype(F32)
+        hot = hit.astype(BF16)
+        position = 2.0 * jnp.dot(high, hot, preferred_element_type=F32) + jnp.dot(low, hot, preferred_element_type=F32)
+        w = weight_ref[at, :]
+        first = w.astype(BF16)
+        over = w - first.astype(F32)
+        second = over.astype(BF16)
+        third = (over - second.astype(F32)).astype(BF16)
+        value = jnp.sum((spread(first) + spread(second) + spread(third)) * hit, axis=0, keepdims=True)
+        meta_ref[d] = jnp.where(top_row == 0, position, jnp.broadcast_to(value, (8, pairs)))
+        return carry
+
+    lax.fori_loop(0, devices, table, 0)
+
+
+def moe_kernel(nx, ny, x_ref, ids_ref, gate_ref, wg_ref, wu_ref, wd_ref, out_ref, tok_ref, h_ref, w_ref,
+               metav, meta_ref, slot_ref, weight_ref, rb, db, ms, mr, ty_s, ty_r, tx_s, tx_r, td_s, td_r, hd_s, hd_r, hf_s, hf_r,
                wa_s, wa_r, wb_s, wb_r, wf_s, wf_r, rs_r, db_r, of_r, credit):
     rows, width = x_ref.shape
     half = rows // 2
@@ -198,9 +232,6 @@
         meta_copy(d).start()
         return carry
 
-    lax.fori_loop(1, ny * eps, meta_send, 0)
-    metav[me] = meta_ref[ep]
-
     def own(dxm, q):
         return tok_ref.at[(x + dxm) % nx, yq[q], c]
 
@@ -235,15 +266,15 @@
         block = w_ref.at[k, ya, pl.ds(g * ep_piece, ep_piece)]
         return remote(block, block, wf_s.at[k, g], wf_r.at[k, g], dev_b)
 
-    def hd(i):
+    def hd(i, s):
         dxm, q = order_of(i)
-        block = h_ref.at[y, (x + dxm) % nx, yq[q]]
-        return remote(block, block, hd_s.at[i], hd_r.at[i], dev_a if q < 2 else dev_b)
-
-    def hf(i):
+        block = h_ref.at[y, (x + dxm) % nx, yq[q], either(s)]
+        return remote(block, block, hd_s.at[i, s], hd_r.at[i, s], dev_a if q < 2 else dev_b)
+
+    def hf(i, s):
         dxm, q = order_of(i)
-        block = h_ref.at[yb, (x + dxm) % nx, place(yb, q)]
-        return remote(block, block, hf_s.at[i], hf_r.at[i], dev_a)
+        block = h_ref.at[yb, (x + dxm) % nx, place(yb, q), either(s)]
+        return remote(block, block, hf_s.at[i, s], hf_r.at[i, s], dev_a)
 
     def send(actions, load_w=None):
         for action in actions:
@@ -261,6 +292,9 @@
         ty(n).start()
         tx(S, n).start()
     td(S, 0).start()
+    routing_tables(ids_ref, gate_ref, meta_ref, slot_ref, weight_ref, per)
+    lax.fori_loop(1, ny * eps, meta_send, 0)
+    metav[me] = meta_ref[ep]
     send(SEND_START)
 
     def came(q):
@@ -348,10 +382,12 @@
                 other.start()
                 meta_wait(lin(xs, ys, c))
 
-            remote(tok_ref.at[xs, ys, c], tok_ref.at[xs, ys, c], td_s.at[q, dxm], td_r.at[q, dxm], dev_p).wait_recv()
-            theirs.start()
-            meta_wait(lin(xs, ys, 1 - c))
             for s in (0, 1):
+                if s == 1:
+                    block = tok_ref.at[xs, ys, c]
+                    remote(block, block, td_s.at[q, dxm], td_r.at[q, dxm], dev_p).wait_recv()
+                    theirs.start()
+                    meta_wait(lin(xs, ys, 1 - c))
                 (other, theirs)[s].wait()
                 hot = one_hot(lin(xs, ys, either(s)))
                 step = min(512, width)
@@ -409,11 +445,17 @@
     def phase_two(wv, hv, gc, o3, pb, pp, sb, fb, wl, hvl, pp_s, rs_s, of_s, ol):
         lane = gc.shape[3]
 
-        def clear(i, carry):
-            wv[i // 8, pl.ds(pl.multiple_of(i % 8 * (deep // 8), 16), deep // 8)] = jnp.zeros((deep // 8, cw), BF16)
+        def clear(k, carry):
+            for e in range(el):
+                low, high = window(e)
+                for q in (S, A, B, O):
+                    at = offset(e, q) + LANES
+                    for start, stop in ((0, e * rest - low), ((e + 1) * rest - low, high - low)):
+                        if stop > start:
+                            wv[k, at + start:at + stop] = jnp.zeros((stop - start, cw), BF16)
             return carry
 
-        lax.fori_loop(0, 8 * kc, clear, 0)
+        lax.fori_loop(0, kc, clear, 0)
 
         def blocks(j):
             return ((x + 2 * nx - 1 - j) % nx, (x + 1 + j) % nx), (y, ya)
@@ -452,10 +494,11 @@
 
         def first_use(j):
             minus, plus = (3 - j) % 4, (1 + j) % 4
-            hd(BATCH[(minus, A)]).wait_recv()
-            hd(BATCH[(plus, S)]).wait_recv()
-            hf(BATCH[(minus, O)]).wait_recv()
-            hf(BATCH[(plus, B)]).wait_recv()
+            for s in (0, 1):
+                hd(BATCH[(minus, A)], s).wait_recv()
+                hd(BATCH[(plus, S)], s).wait_recv()
+                hf(BATCH[(minus, O)], s).wait_recv()
+                hf(BATCH[(plus, B)], s).wait_recv()
 
         def partner_copy(n, d):
             return remote(pp.at[n % 2, d], db.at[n % 2, d], pp_s.at[n % 2, d], db_r.at[n % 2, d], dev_p)
@@ -663,9 +706,10 @@
             wb(k, g).wait_send()
             wf(k, g).wait_send()
     for i in range(16):
-        hd(i).wait_send()
-        if order_of(i)[1] >= 2:
-            hf(i).wait_send()
+        for s in (0, 1):
+            hd(i, s).wait_send()
+            if order_of(i)[1] >= 2:
+                hf(i, s).wait_send()
 
 
 def solution(mesh):
@@ -682,9 +726,6 @@
         per = rows * ids.shape[1] // experts
         pairs = el * per
         cw = width // 2 // CHUNKS
-        position, value = routing_tables(ids, gates, experts, per)
-        meta = jnp.stack([position.reshape(eps, pairs), value.reshape(eps, pairs)], axis=1)
-        meta = jnp.pad(meta, ((0, 0), (0, 6), (0, 0)))
         hbm = pl.BlockSpec(memory_space=pl.ANY)
         vmem = pl.BlockSpec(memory_space=pltpu.VMEM)
         dma = pltpu.SemaphoreType.DMA
@@ -697,23 +738,26 @@
                 jax.ShapeDtypeStruct((ny, nx, ny, 2, el * ff // LANES, per, LANES), BF16),
                 jax.ShapeDtypeStruct((CHUNKS, ny, el, ff, cw), BF16),
             ],
-            in_specs=[hbm, vmem, hbm, hbm, hbm],
+            in_specs=[hbm, vmem, vmem, hbm, hbm, hbm],
             out_specs=[hbm] * 4,
             scratch_shapes=[
                 pltpu.VMEM((ny * eps, 8, pairs), F32),
+                pltpu.VMEM((eps, 8, pairs), F32),
+                pltpu.VMEM((experts, rows), F32),
+                pltpu.VMEM((experts, rows), F32),
                 pltpu.VMEM((2, CHUNKS, 3, rows, cw), F32),
                 pltpu.VMEM((2, 2, rows, cw), F32),
                 dma((ny * eps,)), dma((ny * eps,)),
                 dma((4,)), dma((4,)),
                 dma((4, 4)), dma((4, 4)),
                 dma((4, 4)), dma((4, 4)),
-                dma((16,)), dma((16,)), dma((16,)), dma((16,)),
+                dma((16, 2)), dma((16, 2)), dma((16, 2)), dma((16, 2)),
             ] + [dma((CHUNKS, PIECES))] * 6 + [
                 dma((2, CHUNKS, 3)), dma((2, 2)), dma((CHUNKS,)),
                 pltpu.SemaphoreType.REGULAR,
             ],
             compiler_params=pltpu.CompilerParams(collective_id=0, has_side_effects=True, vmem_limit_bytes=67 * 1000 * 1000),
-        )(x, meta, jnp.transpose(w_gate, (0, 2, 1)), jnp.transpose(w_up, (0, 2, 1)), w_down)
+        )(x, ids.T, gates.T, jnp.transpose(w_gate, (0, 2, 1)), jnp.transpose(w_up, (0, 2, 1)), w_down)
         return outs[0]
 
     return jax.shard_map(

time: 478 us -> 478 us (level)
  no operation moved by 1% of the time
where the time goes in v4:
time: 478 us; the launch traced here: 476 us
  Pallas kernels  473 us (99%)
    pallas_call x1, Pallas kernels, local_moe(): pl.pallas_call(functools.partial(moe_kernel, nx, ny), name='moe_kernel',...  473 us

profile of v4, /device:TPU:97, one launch (start us, length us, event | category | flops | bytes accessed | tf_op | source)
XLA Modules:
  0.0 476.0 jit_solution(11237229170680508621)
XLA Ops:
  0.0 472.8 %moe_kernel.1 = (bf16[512,2048]{1,0:T(8,128)(2,1)}, bf16[4,4,2,512,2048]{4,3,2,1,0:T(8,128)(2,1)}, bf16[4,4,4,2,11,48,256]{6,5,4,3,2,1,0:T(8,128)(2,1)}, bf16[4,4,8,352,256]{4,3,2,1,0:T(8,128)(2,1)}) custom-call(bf16[512,2048]{1,0:T(8,128)(2,1)} %x_ref.1, s32[6,512]{1,0:T(8,128)} %bitcast.6, f32[6,512]{1,0:T(8,128)} %bitcast.7, ...), custom_call_target="tpu_custom_call" | custom-call | tf_op jit(solution)/shard_map/moe_kernel/pallas_call | solution.py:732
  472.8 3.2 copy.8

commit v5 on v4

--- a/solution.py
+++ b/solution.py
@@ -16,28 +16,28 @@
 
 S, A, B, O = 0, 1, 2, 3
 
-UNITS = ((1, 0), (2, 0), (0, 0), (1, 1), (0, 1), (2, 1), (1, 2), (3, 0), (2, 2), (3, 1), (0, 2), (1, 3), (3, 2), (2, 3), (0, 3), (3, 3), )
-ORDER = ((0, 0), (0, 1), (1, 0), (0, 2), (1, 1), (1, 2), (0, 3), (0, 4), (1, 3), (0, 5), (1, 4), (0, 6), (1, 5), (1, 6), (0, 7), (0, 8), (1, 7), (0, 9), (1, 8), (0, 10), (1, 9), (0, 11), (1, 10), (0, 12), (1, 11), (0, 13), (1, 12), (0, 14), (1, 13), (0, 15), (1, 14), (1, 15), )
-OPPOSITE_VIA_A = 3
-OPPOSITE = (2, 3)
-SEND_START = (('wa', 1, 0), ('wb', 2, 1), ('wb', 0, 1), ('wb', 2, 0), )
+UNITS = ((2, 0), (1, 0), (0, 0), (2, 1), (0, 1), (1, 1), (0, 2), (3, 0), (1, 2), (3, 1), (2, 2), (1, 3), (3, 2), (0, 3), (2, 3), (3, 3), )
+ORDER = ((0, 0), (0, 1), (1, 0), (0, 2), (1, 1), (1, 2), (0, 3), (0, 4), (1, 3), (1, 4), (0, 5), (0, 6), (1, 5), (1, 6), (0, 7), (0, 8), (1, 7), (0, 9), (1, 8), (0, 10), (1, 9), (1, 10), (0, 11), (0, 12), (1, 11), (0, 13), (1, 12), (0, 14), (1, 13), (0, 15), (1, 14), (1, 15), )
+OPPOSITE_VIA_A = 4
+OPPOSITE = (2,)
+SEND_START = (('wa', 1, 1), ('wb', 3, 1), ('wb', 1, 0), )
 SEND_BEFORE = (
     (),
     (),
-    (('hd', 1, 1), ('wf', 1, 0), ('wb', 1, 0), ('wb', 1, 1), ),
-    (('hd', 2, 0), ('wa', 0, 1), ('wa', 2, 1), ('wa', 2, 0), ('wa', 0, 0), ('wa', 1, 1), ('wa', 3, 0), ('wa', 3, 1), ),
-    (),
-    (),
-    (('hd', 5, 1), ('hd', 1, 0), ('wf', 0, 1), ),
-    (),
-    (('hd', 7, 0), ('hd', 7, 1), ),
-    (('hd', 8, 0), ('hd', 8, 1), ('wf', 2, 1), ('wf', 2, 0), ),
-    (),
-    (('hf', 8, 1), ('hf', 7, 1), ('hd', 5, 0), ('hf', 7, 0), ('hf', 8, 0), ('hd', 10, 1), ('hd', 10, 0), ),
-    (('hd', 11, 0), ('hd', 11, 1), ('wf', 0, 0), ('wf', 1, 1), ('wb', 0, 0), ),
-    (),
-    (('hf', 11, 0), ('hd', 12, 0), ('hf', 10, 0), ('hf', 11, 1), ('hd', 13, 1), ('hd', 12, 1), ('hd', 13, 0), ('hf', 10, 1), ),
-    (('hd', 14, 0), ('hd', 14, 1), ),
+    (('hd', 1), ('wa', 2, 0), ('wa', 0, 1), ('wa', 2, 1), ('wa', 3, 0), ('wa', 1, 0), ('wa', 0, 0), ('wf', 1, 1), ('wb', 2, 0), ('wb', 0, 0), ('wb', 0, 1), ('wb', 1, 1), ('wb', 2, 1), ),
+    (),
+    (),
+    (),
+    (),
+    (('wf', 2, 0), ),
+    (),
+    (('hd', 8), ('hd', 7), ('wf', 0, 1), ),
+    (),
+    (('hf', 8), ('wa', 3, 1), ('hd', 5), ('wf', 1, 0), ),
+    (('hd', 11), ('hd', 10), ('wf', 0, 0), ('wf', 2, 1), ),
+    (('hd', 12), ('hf', 7), ),
+    (('hf', 11), ('hd', 13), ),
+    (('hf', 10), ('hd', 14), ),
 )
 SEND_AFTER = (
     (),
@@ -57,17 +57,17 @@
     (),
     (),
 )
-SEND_END = (('hf', 14, 0), ('hd', 15, 1), ('hd', 15, 0), ('wf', 3, 1), ('wf', 3, 0), ('wb', 3, 1), ('wb', 3, 0), ('hd', 6, 0), ('hd', 9, 1), ('hd', 6, 1), ('hd', 9, 0), ('lw', 0), ('lw', 1), ('lw', 2), )
+SEND_END = (('hd', 15), ('wf', 3, 1), ('hd', 9), ('wf', 3, 0), ('wb', 3, 0), ('hd', 6), ('lw', 0), ('lw', 1), ('lw', 2), )
 SEND_MAKE = (
     (),
-    (('hf', 14, 1), ),
+    (('hf', 14), ),
     (),
     (),
     (),
     (),
     (),
     (('lw', 3), ),
-    (('hf', 6, 0), ),
+    (),
     (),
     (),
     (),
@@ -77,16 +77,16 @@
     (),
 )
 SEND_JOIN = (
-    (('hf', 15, 1), ),
-    (('hf', 15, 0), ('hd', 4, 0), ('hd', 2, 1), ('hd', 3, 0), ('hd', 0, 0), ('hd', 4, 1), ('hd', 0, 1), ('hd', 3, 1), ),
-    (),
-    (),
-    (),
-    (),
-    (),
-    (('hf', 9, 1), ),
-    (('hf', 6, 1), ),
-    (('hf', 9, 0), ),
+    (),
+    (('hf', 15), ('hd', 2), ('hd', 4), ('hd', 0), ('hd', 3), ),
+    (),
+    (('hf', 9), ),
+    (),
+    (),
+    (),
+    (('hf', 6), ),
+    (),
+    (),
     (),
     (),
     (),
@@ -266,15 +266,15 @@
         block = w_ref.at[k, ya, pl.ds(g * ep_piece, ep_piece)]
         return remote(block, block, wf_s.at[k, g], wf_r.at[k, g], dev_b)
 
-    def hd(i, s):
+    def hd(i):
         dxm, q = order_of(i)
-        block = h_ref.at[y, (x + dxm) % nx, yq[q], either(s)]
-        return remote(block, block, hd_s.at[i, s], hd_r.at[i, s], dev_a if q < 2 else dev_b)
-
-    def hf(i, s):
+        block = h_ref.at[y, (x + dxm) % nx, yq[q]]
+        return remote(block, block, hd_s.at[i], hd_r.at[i], dev_a if q < 2 else dev_b)
+
+    def hf(i):
         dxm, q = order_of(i)
-        block = h_ref.at[yb, (x + dxm) % nx, place(yb, q), either(s)]
-        return remote(block, block, hf_s.at[i, s], hf_r.at[i, s], dev_a)
+        block = h_ref.at[yb, (x + dxm) % nx, place(yb, q)]
+        return remote(block, block, hf_s.at[i], hf_r.at[i], dev_a)
 
     def send(actions, load_w=None):
         for action in actions:
@@ -494,11 +494,10 @@
 
         def first_use(j):
             minus, plus = (3 - j) % 4, (1 + j) % 4
-            for s in (0, 1):
-                hd(BATCH[(minus, A)], s).wait_recv()
-                hd(BATCH[(plus, S)], s).wait_recv()
-                hf(BATCH[(minus, O)], s).wait_recv()
-                hf(BATCH[(plus, B)], s).wait_recv()
+            hd(BATCH[(minus, A)]).wait_recv()
+            hd(BATCH[(plus, S)]).wait_recv()
+            hf(BATCH[(minus, O)]).wait_recv()
+            hf(BATCH[(plus, B)]).wait_recv()
 
         def partner_copy(n, d):
             return remote(pp.at[n % 2, d], db.at[n % 2, d], pp_s.at[n % 2, d], db_r.at[n % 2, d], dev_p)
@@ -706,10 +705,9 @@
             wb(k, g).wait_send()
             wf(k, g).wait_send()
     for i in range(16):
-        for s in (0, 1):
-            hd(i, s).wait_send()
-            if order_of(i)[1] >= 2:
-                hf(i, s).wait_send()
+        hd(i).wait_send()
+        if order_of(i)[1] >= 2:
+            hf(i).wait_send()
 
 
 def solution(mesh):
@@ -751,7 +749,7 @@
                 dma((4,)), dma((4,)),
                 dma((4, 4)), dma((4, 4)),
                 dma((4, 4)), dma((4, 4)),
-                dma((16, 2)), dma((16, 2)), dma((16, 2)), dma((16, 2)),
+                dma((16,)), dma((16,)), dma((16,)), dma((16,)),
             ] + [dma((CHUNKS, PIECES))] * 6 + [
                 dma((2, CHUNKS, 3)), dma((2, 2)), dma((CHUNKS,)),
                 pltpu.SemaphoreType.REGULAR,

time: 478 us -> 473 us (0.990)
  Pallas kernels: 473 us -> 468 us
    pallas_call x1, Pallas kernels: 473 us -> 468 us  [local_moe(): pl.pallas_call(functools.partial(moe_kernel, nx, ny), name='moe_kernel',...]
where the time goes in v5:
time: 473 us; the launch traced here: 471 us
  Pallas kernels  468 us (99%)
    pallas_call x1, Pallas kernels, local_moe(): pl.pallas_call(functools.partial(moe_kernel, nx, ny), name='moe_kernel',...  468 us

profile of v5, /device:TPU:97, one launch (start us, length us, event | category | flops | bytes accessed | tf_op | source)
XLA Modules:
  0.0 470.8 jit_solution(9222391396172782774)
XLA Ops:
  0.0 467.7 %moe_kernel.1 = (bf16[512,2048]{1,0:T(8,128)(2,1)}, bf16[4,4,2,512,2048]{4,3,2,1,0:T(8,128)(2,1)}, bf16[4,4,4,2,11,48,256]{6,5,4,3,2,1,0:T(8,128)(2,1)}, bf16[4,4,8,352,256]{4,3,2,1,0:T(8,128)(2,1)}) custom-call(bf16[512,2048]{1,0:T(8,128)(2,1)} %x_ref.1, s32[6,512]{1,0:T(8,128)} %bitcast.6, f32[6,512]{1,0:T(8,128)} %bitcast.7, ...), custom_call_target="tpu_custom_call" | custom-call | tf_op jit(solution)/shard_map/moe_kernel/pallas_call | solution.py:730
  467.7 3.2 copy.8

commit v6 on v5

--- a/solution.py
+++ b/solution.py
@@ -172,7 +172,7 @@
 
 
 def moe_kernel(nx, ny, x_ref, ids_ref, gate_ref, wg_ref, wu_ref, wd_ref, out_ref, tok_ref, h_ref, w_ref,
-               metav, meta_ref, slot_ref, weight_ref, rb, db, ms, mr, ty_s, ty_r, tx_s, tx_r, td_s, td_r, hd_s, hd_r, hf_s, hf_r,
+               metav, meta_ref, slot_ref, weight_ref, rb, db, ms, mr, ty_s, ty_r, tx_s, tx_r, td_s, td_r, te_s, te_r, hd_s, hd_r, hf_s, hf_r,
                wa_s, wa_r, wb_s, wb_r, wf_s, wf_r, rs_r, db_r, of_r, credit):
     rows, width = x_ref.shape
     half = rows // 2
@@ -248,11 +248,17 @@
     def tx(q, n):
         if n < 2:
             return remote(x_ref if q == S else own(0, q), own(0, q), tx_s.at[q, n], tx_r.at[q, n], (dev_xp, dev_xm)[n])
-        block = rows_of(own((3, 1)[n - 2], q), n - 2)
-        return remote(block, block, tx_s.at[q, n], tx_r.at[q, n], (dev_xp, dev_xm)[n - 2])
+        block = rows_of(own((3, 1)[n % 2], q), n % 2)
+        if q == O:
+            block = block.at[pl.ds((n // 2 - 1) * (half // 2), half // 2)]
+        return remote(block, block, tx_s.at[q, n], tx_r.at[q, n], (dev_xp, dev_xm)[n % 2])
 
     def td(q, dxm):
         return remote(x_ref if (q == S and dxm == 0) else own(dxm, q), own(dxm, q), td_s.at[q, dxm], td_r.at[q, dxm], dev_p)
+
+    def td_last(n):
+        block = rows_of(own(2, O), n % 2).at[pl.ds(n // 2 * (half // 2), half // 2)]
+        return remote(block, block, te_s.at[n], te_r.at[n], dev_p)
 
     def wa(k, g):
         src = wd_ref.at[pl.ds(g * ep_piece, ep_piece), :, pl.ds(pl.multiple_of(cola + k * cw, cw), cw)]
@@ -330,10 +336,16 @@
             q = {7: B, 10: O}[step]
             came(q)
             both(q, 2)
-        if step >= 12:
+            if q == O:
+                both(q, 4)
+        if 12 <= step < 15:
             tx(step - 12, 2).wait_recv()
             tx(step - 12, 3).wait_recv()
             td(step - 12, 2).start()
+        if step == 15:
+            for n in range(4):
+                tx(O, 2 + n).wait_recv()
+                td_last(n).start()
 
     row_id = lax.broadcasted_iota(jnp.int32, (rows, pairs), 0)
 
@@ -384,8 +396,16 @@
 
             for s in (0, 1):
                 if s == 1:
-                    block = tok_ref.at[xs, ys, c]
-                    remote(block, block, td_s.at[q, dxm], td_r.at[q, dxm], dev_p).wait_recv()
+                    @pl.when(i < 15)
+                    def _():
+                        block = tok_ref.at[xs, ys, c]
+                        remote(block, block, td_s.at[q, dxm], td_r.at[q, dxm], dev_p).wait_recv()
+
+                    @pl.when(i == 15)
+                    def _():
+                        for n in range(4):
+                            td_last(n).wait_recv()
+
                     theirs.start()
                     meta_wait(lin(xs, ys, 1 - c))
                 (other, theirs)[s].wait()
@@ -431,6 +451,32 @@
         pltpu.SemaphoreType.DMA((1,)),
     )
 
+    def all_sent():
+        def meta_done(d, carry):
+            meta_copy(d).wait_send()
+            return carry
+
+        lax.fori_loop(1, ny * eps, meta_done, 0)
+        for n in (0, 1) + OPPOSITE:
+            ty(n).wait_send()
+        for q in (S, A, B, O):
+            for n in range(6 if q == O else 4):
+                tx(q, n).wait_send()
+            for dxm in range(4):
+                if (dxm, q) != (2, O):
+                    td(q, dxm).wait_send()
+        for n in range(4):
+            td_last(n).wait_send()
+        for k in range(kc):
+            for g in range(PIECES):
+                wa(k, g).wait_send()
+                wb(k, g).wait_send()
+                wf(k, g).wait_send()
+        for i in range(16):
+            hd(i).wait_send()
+            if order_of(i)[1] >= 2:
+                hf(i).wait_send()
+
     def window(e):
         return e * rest // 128 * 128, -(-(e + 1) * rest // 128) * 128
 
@@ -445,7 +491,7 @@
     def phase_two(wv, hv, gc, o3, pb, pp, sb, fb, wl, hvl, pp_s, rs_s, of_s, ol):
         lane = gc.shape[3]
 
-        def clear(k, carry):
+        def clear(k):
             for e in range(el):
                 low, high = window(e)
                 for q in (S, A, B, O):
@@ -453,9 +499,6 @@
                     for start, stop in ((0, e * rest - low), ((e + 1) * rest - low, high - low)):
                         if stop > start:
                             wv[k, at + start:at + stop] = jnp.zeros((stop - start, cw), BF16)
-            return carry
-
-        lax.fori_loop(0, kc, clear, 0)
 
         def blocks(j):
             return ((x + 2 * nx - 1 - j) % nx, (x + 1 + j) % nx), (y, ya)
@@ -481,6 +524,7 @@
                 wf(k, g).wait_recv()
             for copy in w_loads(k):
                 copy.start()
+            clear(k)
 
         def h_loads(n, j):
             xs, ys = blocks(j)
@@ -532,6 +576,11 @@
             for copy in h_loads(n, j):
                 copy.wait()
 
+            @pl.when(n == 0)
+            def _():
+                later = [action for action in SEND_END + SEND_MAKE[0] if action[0] == 'lw' and action[1] != UNITS[0][0]]
+                send(later, load_w)
+
             for e in range(el):
                 low, high = window(e)
                 parts = []
@@ -608,19 +657,18 @@
                         local, away = out_copies(order % 2, kk)
                         local.wait()
                         away.wait_send()
-                    for d in (0, 1):
+                    local, away = out_copies(order % 2, kk)
+                    for d in (1, 0):
                         ring_copy(0, d, kk, 2).wait_recv()
                         fb[order % 2, d] = (pb[at % 2, d] + db[at % 2, d] + rb[d, kk, 2]).astype(BF16)
-                    local, away = out_copies(order % 2, kk)
-                    local.start()
-                    away.start()
+                        (local, away)[d].start()
 
             @pl.when(n < units - 2)
             def _():
                 pl.semaphore_signal(credit, inc=1, device_id=dev_p, device_id_type=MESH)
 
-        send([action for action in SEND_END if action[0] == 'lw'], load_w)
-        send(SEND_MAKE[0], load_w)
+        send([action for action in SEND_MAKE[0] if action[0] != 'lw'])
+        load_w(UNITS[0][0])
         first_use(UNITS[0][1])
         for copy in h_loads(0, UNITS[0][1]):
             copy.start()
@@ -663,6 +711,7 @@
             local, away = out_copies(slot, 0)
             local.wait()
             away.wait_send()
+        all_sent()
         for k in range(kc):
             out_copies(0, k)[1].wait_recv()
 
@@ -686,28 +735,6 @@
         pltpu.SemaphoreType.DMA((2,)),
         pltpu.SemaphoreType.DMA((2,)),
     )
-
-    def meta_done(d, carry):
-        meta_copy(d).wait_send()
-        return carry
-
-    lax.fori_loop(1, ny * eps, meta_done, 0)
-    for n in (0, 1) + OPPOSITE:
-        ty(n).wait_send()
-    for q in (S, A, B, O):
-        for n in range(4):
-            tx(q, n).wait_send()
-        for dxm in range(4):
-            td(q, dxm).wait_send()
-    for k in range(kc):
-        for g in range(PIECES):
-            wa(k, g).wait_send()
-            wb(k, g).wait_send()
-            wf(k, g).wait_send()
-    for i in range(16):
-        hd(i).wait_send()
-        if order_of(i)[1] >= 2:
-            hf(i).wait_send()
 
 
 def solution(mesh):
@@ -747,8 +774,8 @@
                 pltpu.VMEM((2, 2, rows, cw), F32),
                 dma((ny * eps,)), dma((ny * eps,)),
                 dma((4,)), dma((4,)),
-                dma((4, 4)), dma((4, 4)),
-                dma((4, 4)), dma((4, 4)),
+                dma((4, 6)), dma((4, 6)),
+                dma((4, 4)), dma((4, 4)), dma((4,)), dma((4,)),
                 dma((16,)), dma((16,)), dma((16,)), dma((16,)),
             ] + [dma((CHUNKS, PIECES))] * 6 + [
                 dma((2, CHUNKS, 3)), dma((2, 2)), dma((CHUNKS,)),

time: 473 us -> 473 us (level)
  no operation moved by 1% of the time
where the time goes in v6:
time: 473 us; the launch traced here: 471 us
  Pallas kernels  468 us (99%)
    pallas_call x1, Pallas kernels, local_moe(): pl.pallas_call(functools.partial(moe_kernel, nx, ny), name='moe_kernel',...  468 us

profile of v6, /device:TPU:97, one launch (start us, length us, event | category | flops | bytes accessed | tf_op | source)
XLA Modules:
  0.0 471.1 jit_solution(14574715770812804763)
XLA Ops:
  0.0 467.9 %moe_kernel.1 = (bf16[512,2048]{1,0:T(8,128)(2,1)}, bf16[4,4,2,512,2048]{4,3,2,1,0:T(8,128)(2,1)}, bf16[4,4,4,2,11,48,256]{6,5,4,3,2,1,0:T(8,128)(2,1)}, bf16[4,4,8,352,256]{4,3,2,1,0:T(8,128)(2,1)}) custom-call(bf16[512,2048]{1,0:T(8,128)(2,1)} %x_ref.1, s32[6,512]{1,0:T(8,128)} %bitcast.6, f32[6,512]{1,0:T(8,128)} %bitcast.7, ...), custom_call_target="tpu_custom_call" | custom-call | tf_op jit(solution)/shard_map/moe_kernel/pallas_call | solution.py:757
  468.0 3.2 copy.8

commit v7 on v6

--- a/solution.py
+++ b/solution.py
@@ -16,28 +16,28 @@
 
 S, A, B, O = 0, 1, 2, 3
 
-UNITS = ((2, 0), (1, 0), (0, 0), (2, 1), (0, 1), (1, 1), (0, 2), (3, 0), (1, 2), (3, 1), (2, 2), (1, 3), (3, 2), (0, 3), (2, 3), (3, 3), )
-ORDER = ((0, 0), (0, 1), (1, 0), (0, 2), (1, 1), (1, 2), (0, 3), (0, 4), (1, 3), (1, 4), (0, 5), (0, 6), (1, 5), (1, 6), (0, 7), (0, 8), (1, 7), (0, 9), (1, 8), (0, 10), (1, 9), (1, 10), (0, 11), (0, 12), (1, 11), (0, 13), (1, 12), (0, 14), (1, 13), (0, 15), (1, 14), (1, 15), )
+UNITS = ((0, 0), (1, 0), (2, 0), (0, 1), (1, 1), (2, 1), (0, 2), (3, 0), (2, 2), (3, 1), (1, 2), (3, 2), (2, 3), (1, 3), (0, 3), (3, 3), )
+ORDER = ((0, 0), (1, 0), (0, 1), (0, 2), (1, 1), (1, 2), (0, 3), (0, 4), (1, 3), (1, 4), (0, 5), (0, 6), (1, 5), (1, 6), (0, 7), (1, 7), (0, 8), (0, 9), (1, 8), (0, 10), (1, 9), (1, 10), (0, 11), (0, 12), (1, 11), (0, 13), (1, 12), (0, 14), (1, 13), (0, 15), (1, 14), (1, 15), )
 OPPOSITE_VIA_A = 4
 OPPOSITE = (2,)
-SEND_START = (('wa', 1, 1), ('wb', 3, 1), ('wb', 1, 0), )
+SEND_START = (('wa', 2, 1), ('wb', 2, 1), )
 SEND_BEFORE = (
     (),
     (),
-    (('hd', 1), ('wa', 2, 0), ('wa', 0, 1), ('wa', 2, 1), ('wa', 3, 0), ('wa', 1, 0), ('wa', 0, 0), ('wf', 1, 1), ('wb', 2, 0), ('wb', 0, 0), ('wb', 0, 1), ('wb', 1, 1), ('wb', 2, 1), ),
-    (),
-    (),
-    (),
+    (('wf', 2, 1), ('wb', 1, 0), ('wb', 0, 1), ('wb', 2, 0), ('wb', 1, 1), ('wb', 0, 0), ),
+    (('hd', 2), ('wa', 3, 0), ('wa', 2, 0), ('wa', 0, 0), ('wa', 1, 0), ),
+    (),
+    (),
+    (('hd', 5), ('wa', 0, 1), ('wa', 1, 1), ('hd', 1), ),
     (),
     (('wf', 2, 0), ),
-    (),
-    (('hd', 8), ('hd', 7), ('wf', 0, 1), ),
-    (),
-    (('hf', 8), ('wa', 3, 1), ('hd', 5), ('wf', 1, 0), ),
-    (('hd', 11), ('hd', 10), ('wf', 0, 0), ('wf', 2, 1), ),
-    (('hd', 12), ('hf', 7), ),
-    (('hf', 11), ('hd', 13), ),
-    (('hf', 10), ('hd', 14), ),
+    (('hd', 8), ('hd', 7), ),
+    (),
+    (('hf', 7), ('hf', 8), ('hd', 10), ),
+    (('hd', 11), ),
+    (),
+    (('hd', 13), ('hd', 12), ),
+    (('hf', 11), ('hf', 10), ('hd', 14), ),
 )
 SEND_AFTER = (
     (),
@@ -50,24 +50,24 @@
     (),
     (),
     (),
-    (),
-    (),
-    (),
-    (),
+    (('wf', 1, 0), ('wf', 0, 0), ),
+    (),
+    (),
+    (('wf', 1, 1), ('wf', 0, 1), ),
     (),
     (),
 )
-SEND_END = (('hd', 15), ('wf', 3, 1), ('hd', 9), ('wf', 3, 0), ('wb', 3, 0), ('hd', 6), ('lw', 0), ('lw', 1), ('lw', 2), )
+SEND_END = (('hd', 15), ('wb', 3, 1), ('wf', 3, 0), ('wb', 3, 0), ('lw', 0), ('lw', 1), ('lw', 2), )
 SEND_MAKE = (
     (),
-    (('hf', 14), ),
-    (),
-    (),
-    (),
-    (),
+    (),
+    (('hf', 15), ('wa', 3, 1), ('hd', 4), ('hd', 0), ('hd', 3), ),
+    (),
+    (),
+    (('wf', 3, 1), ('hd', 6), ('hd', 9), ),
     (),
     (('lw', 3), ),
-    (),
+    (('hf', 6), ),
     (),
     (),
     (),
@@ -77,16 +77,16 @@
     (),
 )
 SEND_JOIN = (
-    (),
-    (('hf', 15), ('hd', 2), ('hd', 4), ('hd', 0), ('hd', 3), ),
+    (('hf', 14), ),
+    (),
+    (),
+    (),
+    (),
+    (),
+    (),
+    (),
     (),
     (('hf', 9), ),
-    (),
-    (),
-    (),
-    (('hf', 6), ),
-    (),
-    (),
     (),
     (),
     (),

time: 473 us -> 475 us (level)
  no operation moved by 1% of the time
where the time goes in v7:
time: 475 us; the launch traced here: 474 us
  Pallas kernels  471 us (99%)
    pallas_call x1, Pallas kernels, local_moe(): pl.pallas_call(functools.partial(moe_kernel, nx, ny), name='moe_kernel',...  471 us

profile of v7, /device:TPU:97, one launch (start us, length us, event | category | flops | bytes accessed | tf_op | source)
XLA Modules:
  0.0 473.9 jit_solution(1428346212200654759)
XLA Ops:
  0.0 470.7 %moe_kernel.1 = (bf16[512,2048]{1,0:T(8,128)(2,1)}, bf16[4,4,2,512,2048]{4,3,2,1,0:T(8,128)(2,1)}, bf16[4,4,4,2,11,48,256]{6,5,4,3,2,1,0:T(8,128)(2,1)}, bf16[4,4,8,352,256]{4,3,2,1,0:T(8,128)(2,1)}) custom-call(bf16[512,2048]{1,0:T(8,128)(2,1)} %x_ref.1, s32[6,512]{1,0:T(8,128)} %bitcast.6, f32[6,512]{1,0:T(8,128)} %bitcast.7, ...), custom_call_target="tpu_custom_call" | custom-call | tf_op jit(solution)/shard_map/moe_kernel/pallas_call | solution.py:757
  470.7 3.2 copy.8

commit v8 on v7

--- a/solution.py
+++ b/solution.py
@@ -16,28 +16,28 @@
 
 S, A, B, O = 0, 1, 2, 3
 
-UNITS = ((0, 0), (1, 0), (2, 0), (0, 1), (1, 1), (2, 1), (0, 2), (3, 0), (2, 2), (3, 1), (1, 2), (3, 2), (2, 3), (1, 3), (0, 3), (3, 3), )
-ORDER = ((0, 0), (1, 0), (0, 1), (0, 2), (1, 1), (1, 2), (0, 3), (0, 4), (1, 3), (1, 4), (0, 5), (0, 6), (1, 5), (1, 6), (0, 7), (1, 7), (0, 8), (0, 9), (1, 8), (0, 10), (1, 9), (1, 10), (0, 11), (0, 12), (1, 11), (0, 13), (1, 12), (0, 14), (1, 13), (0, 15), (1, 14), (1, 15), )
+UNITS = ((1, 0), (0, 0), (2, 0), (0, 1), (2, 1), (1, 1), (0, 2), (3, 0), (2, 2), (3, 1), (1, 2), (2, 3), (3, 2), (0, 3), (1, 3), (3, 3), )
+ORDER = ((0, 0), (1, 0), (0, 1), (1, 1), (0, 2), (0, 3), (1, 2), (0, 4), (1, 3), (1, 4), (0, 5), (1, 5), (0, 6), (0, 7), (1, 6), (0, 8), (1, 7), (0, 9), (1, 8), (0, 10), (1, 9), (0, 11), (1, 10), (0, 12), (1, 11), (0, 13), (1, 12), (0, 14), (1, 13), (0, 15), (1, 14), (1, 15), )
 OPPOSITE_VIA_A = 4
 OPPOSITE = (2,)
-SEND_START = (('wa', 2, 1), ('wb', 2, 1), )
+SEND_START = (('wa', 2, 1), ('wb', 2, 0), ('wb', 0, 0), ('wb', 1, 0), ('wb', 1, 1), )
 SEND_BEFORE = (
     (),
     (),
-    (('wf', 2, 1), ('wb', 1, 0), ('wb', 0, 1), ('wb', 2, 0), ('wb', 1, 1), ('wb', 0, 0), ),
-    (('hd', 2), ('wa', 3, 0), ('wa', 2, 0), ('wa', 0, 0), ('wa', 1, 0), ),
-    (),
-    (),
-    (('hd', 5), ('wa', 0, 1), ('wa', 1, 1), ('hd', 1), ),
-    (),
-    (('wf', 2, 0), ),
-    (('hd', 8), ('hd', 7), ),
-    (),
-    (('hf', 7), ('hf', 8), ('hd', 10), ),
-    (('hd', 11), ),
-    (),
-    (('hd', 13), ('hd', 12), ),
-    (('hf', 11), ('hf', 10), ('hd', 14), ),
+    (('hd', 1), ('wa', 1, 1), ('wa', 0, 1), ('wa', 0, 0), ('wa', 2, 0), ('wa', 1, 0), ('wa', 3, 0), ),
+    (('wf', 2, 1), ('wb', 2, 1), ('wb', 0, 1), ),
+    (),
+    (),
+    (('wf', 1, 1), ),
+    (),
+    (('hd', 7), ),
+    (('hd', 8), ('wf', 0, 0), ('wf', 0, 1), ),
+    (),
+    (('hf', 8), ('hf', 7), ('hd', 5), ),
+    (('hd', 11), ('hd', 10), ('wf', 1, 0), ('wf', 2, 0), ),
+    (),
+    (('hf', 11), ),
+    (('hd', 14), ),
 )
 SEND_AFTER = (
     (),
@@ -50,21 +50,21 @@
     (),
     (),
     (),
-    (('wf', 1, 0), ('wf', 0, 0), ),
-    (),
-    (),
-    (('wf', 1, 1), ('wf', 0, 1), ),
-    (),
+    (),
+    (),
+    (),
+    (),
+    (('hf', 10), ('hd', 13), ('hd', 12), ),
     (),
 )
 SEND_END = (('hd', 15), ('wb', 3, 1), ('wf', 3, 0), ('wb', 3, 0), ('lw', 0), ('lw', 1), ('lw', 2), )
 SEND_MAKE = (
     (),
-    (),
-    (('hf', 15), ('wa', 3, 1), ('hd', 4), ('hd', 0), ('hd', 3), ),
-    (),
-    (),
-    (('wf', 3, 1), ('hd', 6), ('hd', 9), ),
+    (('hf', 15), ('wa', 3, 1), ('hd', 2), ('hd', 4), ('hd', 3), ('hd', 0), ),
+    (),
+    (),
+    (),
+    (),
     (),
     (('lw', 3), ),
     (('hf', 6), ),
@@ -81,12 +81,12 @@
     (),
     (),
     (),
-    (),
-    (),
+    (('wf', 3, 1), ('hd', 6), ('hd', 9), ),
     (),
     (),
     (),
     (('hf', 9), ),
+    (),
     (),
     (),
     (),
@@ -172,7 +172,7 @@
 
 
 def moe_kernel(nx, ny, x_ref, ids_ref, gate_ref, wg_ref, wu_ref, wd_ref, out_ref, tok_ref, h_ref, w_ref,
-               metav, meta_ref, slot_ref, weight_ref, rb, db, ms, mr, ty_s, ty_r, tx_s, tx_r, td_s, td_r, te_s, te_r, hd_s, hd_r, hf_s, hf_r,
+               metav, meta_ref, slot_ref, weight_ref, rb, db, ms, mr, ty_s, ty_r, tx_s, tx_r, td_s, td_r, room, o3, hd_s, hd_r, hf_s, hf_r,
                wa_s, wa_r, wb_s, wb_r, wf_s, wf_r, rs_r, db_r, of_r, credit):
     rows, width = x_ref.shape
     half = rows // 2
@@ -248,17 +248,9 @@
     def tx(q, n):
         if n < 2:
             return remote(x_ref if q == S else own(0, q), own(0, q), tx_s.at[q, n], tx_r.at[q, n], (dev_xp, dev_xm)[n])
-        block = rows_of(own((3, 1)[n % 2], q), n % 2)
-        if q == O:
-            block = block.at[pl.ds((n // 2 - 1) * (half // 2), half // 2)]
-        return remote(block, block, tx_s.at[q, n], tx_r.at[q, n], (dev_xp, dev_xm)[n % 2])
-
-    def td(q, dxm):
-        return remote(x_ref if (q == S and dxm == 0) else own(dxm, q), own(dxm, q), td_s.at[q, dxm], td_r.at[q, dxm], dev_p)
-
-    def td_last(n):
-        block = rows_of(own(2, O), n % 2).at[pl.ds(n // 2 * (half // 2), half // 2)]
-        return remote(block, block, te_s.at[n], te_r.at[n], dev_p)
+        block = rows_of(own((3, 1)[n - 2], q), n - 2)
+        return remote(block, block, tx_s.at[q, n], tx_r.at[q, n], (dev_xp, dev_xm)[n - 2])
+
 
     def wa(k, g):
         src = wd_ref.at[pl.ds(g * ep_piece, ep_piece), :, pl.ds(pl.multiple_of(cola + k * cw, cw), cw)]
@@ -297,7 +289,6 @@
     for n in (0, 1):
         ty(n).start()
         tx(S, n).start()
-    td(S, 0).start()
     routing_tables(ids_ref, gate_ref, meta_ref, slot_ref, weight_ref, per)
     lax.fori_loop(1, ny * eps, meta_send, 0)
     metav[me] = meta_ref[ep]
@@ -306,8 +297,6 @@
     def came(q):
         for n in (0, 1):
             tx(q, n).wait_recv()
-        td(q, 1).start()
-        td(q, 3).start()
 
     def both(q, first):
         tx(q, first).start()
@@ -322,8 +311,6 @@
             both(A, 0)
             both(B, 0)
             came(S)
-            td(A, 0).start()
-            td(B, 0).start()
         if step == 4:
             came(A)
             for n in OPPOSITE:
@@ -331,21 +318,13 @@
             both(O, 0)
             both(S, 2)
             both(A, 2)
-            td(O, 0).start()
         if step in (7, 10):
             q = {7: B, 10: O}[step]
             came(q)
             both(q, 2)
-            if q == O:
-                both(q, 4)
-        if 12 <= step < 15:
+        if step >= 12:
             tx(step - 12, 2).wait_recv()
             tx(step - 12, 3).wait_recv()
-            td(step - 12, 2).start()
-        if step == 15:
-            for n in range(4):
-                tx(O, 2 + n).wait_recv()
-                td_last(n).start()
 
     row_id = lax.broadcasted_iota(jnp.int32, (rows, pairs), 0)
 
@@ -365,6 +344,9 @@
         def store(i):
             dxm, q = order_of(i)
             return pltpu.make_async_copy(hb, h_ref.at[y, (x + dxm) % nx, place(y, q)], hl.at[0])
+
+        def to_partner(m):
+            return remote(tb.at[:, pl.ds(m * cw, cw)], o3.at[pl.ds(m * rows, rows)], td_s.at[m], td_r.at[m], dev_p)
 
         def batch(i, carry):
             @pl.when(i > 0)
@@ -381,9 +363,13 @@
 
             dxm, q = order_of(i)
             xs, ys = (x + dxm) % nx, place(y, q)
-            mine = pltpu.make_async_copy(x_ref, tb.at[0], tl.at[0])
-            other = pltpu.make_async_copy(tok_ref.at[xs, ys, c], tb.at[0], tl.at[0])
-            theirs = pltpu.make_async_copy(tok_ref.at[xs, ys, 1 - c], tb.at[1], tl.at[1])
+            mine = pltpu.make_async_copy(x_ref, tb, tl.at[0])
+            arrived = pltpu.make_async_copy(tok_ref.at[xs, ys, c], tb, tl.at[0])
+
+            @pl.when(i > 0)
+            def _():
+                for m in range(width // cw):
+                    to_partner(m).wait_send()
 
             @pl.when(i == 0)
             def _():
@@ -391,29 +377,28 @@
 
             @pl.when(i > 0)
             def _():
-                other.start()
+                arrived.start()
+                pl.semaphore_wait(room, 1)
                 meta_wait(lin(xs, ys, c))
 
-            for s in (0, 1):
-                if s == 1:
-                    @pl.when(i < 15)
-                    def _():
-                        block = tok_ref.at[xs, ys, c]
-                        remote(block, block, td_s.at[q, dxm], td_r.at[q, dxm], dev_p).wait_recv()
-
-                    @pl.when(i == 15)
-                    def _():
-                        for n in range(4):
-                            td_last(n).wait_recv()
-
-                    theirs.start()
-                    meta_wait(lin(xs, ys, 1 - c))
-                (other, theirs)[s].wait()
-                hot = one_hot(lin(xs, ys, either(s)))
-                step = min(512, width)
-                for lo in range(0, width, step):
-                    got = lax.dot_general(hot, tb[s, :, lo:lo + step], (((0,), (0,)), ((), ())), preferred_element_type=F32)
-                    xg[:, s, :, lo:lo + step] = got.astype(BF16).reshape(el, per, step)
+            arrived.wait()
+            for m in range(width // cw):
+                to_partner(m).start()
+            hot = one_hot(lin(xs, ys, c))
+            step = min(512, width)
+            for lo in range(0, width, step):
+                got = lax.dot_general(hot, tb[:, lo:lo + step], (((0,), (0,)), ((), ())), preferred_element_type=F32)
+                xg[:, 0, :, lo:lo + step] = got.astype(BF16).reshape(el, per, step)
+            meta_wait(lin(xs, ys, 1 - c))
+            hot = one_hot(lin(xs, ys, 1 - c))
+            for m in range(width // cw):
+                to_partner(m).wait_recv()
+                got = lax.dot_general(hot, o3[m * rows:(m + 1) * rows, :], (((0,), (0,)), ((), ())), preferred_element_type=F32)
+                xg[:, 1, :, m * cw:(m + 1) * cw] = got.astype(BF16).reshape(el, per, cw)
+
+            @pl.when(i < 15)
+            def _():
+                pl.semaphore_signal(room, inc=1, device_id=dev_p, device_id_type=MESH)
 
             @pl.when(i == 0)
             def _():
@@ -436,13 +421,15 @@
             return carry
 
         lax.fori_loop(0, 16, batch, 0)
+        for m in range(width // cw):
+            to_partner(m).wait_send()
         store(15).wait()
 
     pl.run_scoped(
         phase_one,
         pltpu.VMEM((el, ff, width), BF16),
         pltpu.VMEM((el, ff, width), BF16),
-        pltpu.VMEM((2, rows, width), BF16),
+        pltpu.VMEM((rows, width), BF16),
         pltpu.VMEM((el, 2, per, width), BF16),
         pltpu.VMEM((2,) + h_ref.shape[4:], BF16),
         pltpu.VMEM((el, 2 * per, rest), F32),
@@ -460,13 +447,8 @@
         for n in (0, 1) + OPPOSITE:
             ty(n).wait_send()
         for q in (S, A, B, O):
-            for n in range(6 if q == O else 4):
+            for n in range(4):
                 tx(q, n).wait_send()
-            for dxm in range(4):
-                if (dxm, q) != (2, O):
-                    td(q, dxm).wait_send()
-        for n in range(4):
-            td_last(n).wait_send()
         for k in range(kc):
             for g in range(PIECES):
                 wa(k, g).wait_send()
@@ -488,7 +470,7 @@
 
     units = len(UNITS)
 
-    def phase_two(wv, hv, gc, o3, pb, pp, sb, fb, wl, hvl, pp_s, rs_s, of_s, ol):
+    def phase_two(wv, hv, gc, pb, pp, sb, fb, wl, hvl, pp_s, rs_s, of_s, ol):
         lane = gc.shape[3]
 
         def clear(k):
@@ -596,9 +578,10 @@
                 over = v - hi.astype(F32)
                 mid = over.astype(BF16)
                 low_part = (over - mid.astype(F32)).astype(BF16)
-                o3[:, 0, e] = hi.reshape(4, per, cw)
-                o3[:, 1, e] = mid.reshape(4, per, cw)
-                o3[:, 2, e] = low_part.reshape(4, per, cw)
+                for m in range(4):
+                    for third, value in enumerate((hi, mid, low_part)):
+                        at = (3 * m + third) * pairs + e * per
+                        o3[at:at + per, :] = value[m * per:(m + 1) * per]
 
             @pl.when(n >= 2)
             def _():
@@ -609,9 +592,10 @@
             for rel in (1, 0):
                 for d in (0, 1):
                     hot = one_hot(lin(xs[d], ys[d], either(rel)))
-                    total = jnp.dot(hot, o3[2 * d + rel, 0].reshape(pairs, cw), preferred_element_type=F32)
-                    total += jnp.dot(hot, o3[2 * d + rel, 1].reshape(pairs, cw), preferred_element_type=F32)
-                    total += jnp.dot(hot, o3[2 * d + rel, 2].reshape(pairs, cw), preferred_element_type=F32)
+                    at = 3 * (2 * d + rel) * pairs
+                    total = jnp.dot(hot, o3[at:at + pairs, :], preferred_element_type=F32)
+                    total += jnp.dot(hot, o3[at + pairs:at + 2 * pairs, :], preferred_element_type=F32)
+                    total += jnp.dot(hot, o3[at + 2 * pairs:at + 3 * pairs, :], preferred_element_type=F32)
                     if rel == 1:
                         pp[n % 2, d] = total
                         partner_copy(n, d).start()
@@ -723,7 +707,6 @@
         pltpu.VMEM((kc, deep, cw), BF16),
         pltpu.VMEM((2, 4, h_ref.shape[4], 4, per, LANES), BF16),
         pltpu.VMEM((el, 4, per, lane), F32),
-        pltpu.VMEM((4, 3, el, per, cw), BF16),
         pltpu.VMEM((2, 2, rows, cw), F32),
         pltpu.VMEM((2, 2, rows, cw), F32),
         pltpu.VMEM((4, 2, rows, cw), F32),
@@ -774,8 +757,9 @@
                 pltpu.VMEM((2, 2, rows, cw), F32),
                 dma((ny * eps,)), dma((ny * eps,)),
                 dma((4,)), dma((4,)),
-                dma((4, 6)), dma((4, 6)),
-                dma((4, 4)), dma((4, 4)), dma((4,)), dma((4,)),
+                dma((4, 4)), dma((4, 4)),
+                dma((width // cw,)), dma((width // cw,)), pltpu.SemaphoreType.REGULAR,
+                pltpu.VMEM((12 * pairs, cw), BF16),
                 dma((16,)), dma((16,)), dma((16,)), dma((16,)),
             ] + [dma((CHUNKS, PIECES))] * 6 + [
                 dma((2, CHUNKS, 3)), dma((2, 2)), dma((CHUNKS,)),

time: 475 us -> 473 us (level)
  no operation moved by 1% of the time
where the time goes in v8:
time: 473 us; the launch traced here: 472 us
  Pallas kernels  469 us (99%)
    pallas_call x1, Pallas kernels, local_moe(): pl.pallas_call(functools.partial(moe_kernel, nx, ny), name='moe_kernel',...  469 us

profile of v8, /device:TPU:97, one launch (start us, length us, event | category | flops | bytes accessed | tf_op | source)
XLA Modules:
  0.0 472.3 jit_solution(2667581847951906402)
XLA Ops:
  0.0 469.2 %moe_kernel.1 = (bf16[512,2048]{1,0:T(8,128)(2,1)}, bf16[4,4,2,512,2048]{4,3,2,1,0:T(8,128)(2,1)}, bf16[4,4,4,2,11,48,256]{6,5,4,3,2,1,0:T(8,128)(2,1)}, bf16[4,4,8,352,256]{4,3,2,1,0:T(8,128)(2,1)}) custom-call(bf16[512,2048]{1,0:T(8,128)(2,1)} %x_ref.1, s32[6,512]{1,0:T(8,128)} %bitcast.6, f32[6,512]{1,0:T(8,128)} %bitcast.7, ...), custom_call_target="tpu_custom_call" | custom-call | tf_op jit(solution)/shard_map/moe_kernel/pallas_call | solution.py:740
  469.2 3.2 copy.8

commit v9 on v8

--- a/solution.py
+++ b/solution.py
@@ -16,28 +16,28 @@
 
 S, A, B, O = 0, 1, 2, 3
 
-UNITS = ((1, 0), (0, 0), (2, 0), (0, 1), (2, 1), (1, 1), (0, 2), (3, 0), (2, 2), (3, 1), (1, 2), (2, 3), (3, 2), (0, 3), (1, 3), (3, 3), )
-ORDER = ((0, 0), (1, 0), (0, 1), (1, 1), (0, 2), (0, 3), (1, 2), (0, 4), (1, 3), (1, 4), (0, 5), (1, 5), (0, 6), (0, 7), (1, 6), (0, 8), (1, 7), (0, 9), (1, 8), (0, 10), (1, 9), (0, 11), (1, 10), (0, 12), (1, 11), (0, 13), (1, 12), (0, 14), (1, 13), (0, 15), (1, 14), (1, 15), )
+UNITS = ((2, 0), (0, 0), (1, 0), (2, 1), (0, 1), (1, 1), (2, 2), (3, 0), (1, 2), (3, 1), (0, 2), (2, 3), (3, 2), (1, 3), (0, 3), (3, 3), )
+ORDER = ((0, 0), (1, 0), (0, 1), (0, 2), (1, 1), (1, 2), (0, 3), (0, 4), (1, 3), (0, 5), (1, 4), (0, 6), (1, 5), (1, 6), (0, 7), (0, 8), (1, 7), (0, 9), (1, 8), (0, 10), (1, 9), (0, 11), (1, 10), (0, 12), (1, 11), (0, 13), (1, 12), (0, 14), (1, 13), (0, 15), (1, 14), (1, 15), )
 OPPOSITE_VIA_A = 4
 OPPOSITE = (2,)
-SEND_START = (('wa', 2, 1), ('wb', 2, 0), ('wb', 0, 0), ('wb', 1, 0), ('wb', 1, 1), )
+SEND_START = (('wa', 1, 0), ('wa', 2, 1), ('wb', 1, 1), ('wb', 2, 0), ('wb', 0, 1), )
 SEND_BEFORE = (
     (),
     (),
-    (('hd', 1), ('wa', 1, 1), ('wa', 0, 1), ('wa', 0, 0), ('wa', 2, 0), ('wa', 1, 0), ('wa', 3, 0), ),
-    (('wf', 2, 1), ('wb', 2, 1), ('wb', 0, 1), ),
-    (),
-    (),
-    (('wf', 1, 1), ),
+    (('hd', 1), ('wa', 0, 0), ),
+    (('wf', 1, 0), ('wb', 2, 1), ('wb', 1, 0), ('wb', 0, 0), ),
+    (('wf', 2, 1), ),
+    (),
+    (('hd', 5), ('wa', 2, 0), ('wa', 0, 1), ('wa', 1, 1), ),
     (),
     (('hd', 7), ),
-    (('hd', 8), ('wf', 0, 0), ('wf', 0, 1), ),
-    (),
-    (('hf', 8), ('hf', 7), ('hd', 5), ),
-    (('hd', 11), ('hd', 10), ('wf', 1, 0), ('wf', 2, 0), ),
-    (),
-    (('hf', 11), ),
-    (('hd', 14), ),
+    (('hd', 8), ('wf', 2, 0), ),
+    (),
+    (('hf', 8), ('hd', 2), ('wf', 0, 1), ),
+    (('wf', 1, 1), ('hd', 11), ('hd', 10), ('wf', 0, 0), ),
+    (('hd', 12), ('hf', 7), ('wa', 3, 1), ),
+    (),
+    (('hf', 11), ('hf', 10), ('hd', 13), ('hd', 14), ),
 )
 SEND_AFTER = (
     (),
@@ -54,17 +54,17 @@
     (),
     (),
     (),
-    (('hf', 10), ('hd', 13), ('hd', 12), ),
+    (),
     (),
 )
-SEND_END = (('hd', 15), ('wb', 3, 1), ('wf', 3, 0), ('wb', 3, 0), ('lw', 0), ('lw', 1), ('lw', 2), )
+SEND_END = (('hd', 15), ('wb', 3, 1), ('wf', 3, 1), ('wb', 3, 0), ('lw', 0), ('lw', 1), ('lw', 2), )
 SEND_MAKE = (
     (),
-    (('hf', 15), ('wa', 3, 1), ('hd', 2), ('hd', 4), ('hd', 3), ('hd', 0), ),
-    (),
-    (),
-    (),
-    (),
+    (('hf', 15), ('wa', 3, 0), ('hd', 4), ('hd', 0), ('hd', 3), ),
+    (),
+    (),
+    (),
+    (('wf', 3, 0), ('hd', 6), ('hd', 9), ),
     (),
     (('lw', 3), ),
     (('hf', 6), ),
@@ -81,7 +81,7 @@
     (),
     (),
     (),
-    (('wf', 3, 1), ('hd', 6), ('hd', 9), ),
+    (),
     (),
     (),
     (),
@@ -102,6 +102,7 @@
 
 
 BATCH = {order_of(i): i for i in range(16)}
+AHEAD = (0, 0, 1, 1, 0, 1, 1, 0, 1, 1, 0, 1, 0, 0, 0, 0)
 FIRST_STEP = {}
 for place_in_order, (chunk_of, step_of) in enumerate(UNITS):
     FIRST_STEP.setdefault(step_of, place_in_order)
@@ -345,8 +346,12 @@
             dxm, q = order_of(i)
             return pltpu.make_async_copy(hb, h_ref.at[y, (x + dxm) % nx, place(y, q)], hl.at[0])
 
-        def to_partner(m):
-            return remote(tb.at[:, pl.ds(m * cw, cw)], o3.at[pl.ds(m * rows, rows)], td_s.at[m], td_r.at[m], dev_p)
+        def rows_in(i):
+            dxm, q = order_of(i)
+            return pltpu.make_async_copy(tok_ref.at[(x + dxm) % nx, place(y, q), c], tb.at[i % 2], tl.at[i % 2])
+
+        def to_partner(i, m):
+            return remote(tb.at[i % 2, :, pl.ds(m * cw, cw)], o3.at[pl.ds(m * rows, rows)], td_s.at[i % 2, m], td_r.at[m], dev_p)
 
         def batch(i, carry):
             @pl.when(i > 0)
@@ -363,42 +368,64 @@
 
             dxm, q = order_of(i)
             xs, ys = (x + dxm) % nx, place(y, q)
-            mine = pltpu.make_async_copy(x_ref, tb, tl.at[0])
-            arrived = pltpu.make_async_copy(tok_ref.at[xs, ys, c], tb, tl.at[0])
+            ahead, next_ahead = look_up(AHEAD, i), look_up(AHEAD[1:] + (0,), i)
+
+            @pl.when(ahead == 0)
+            def _():
+                @pl.when(i >= 2)
+                def _():
+                    for m in range(width // cw):
+                        to_partner(i - 2, m).wait_send()
+
+                @pl.when(i == 0)
+                def _():
+                    pltpu.make_async_copy(x_ref, tb.at[0], tl.at[0]).start()
+
+                @pl.when(i > 0)
+                def _():
+                    rows_in(i).start()
+
+                rows_in(i).wait()
+
+                @pl.when(i > 0)
+                def _():
+                    pl.semaphore_wait(room, 1)
+
+                for m in range(width // cw):
+                    to_partner(i, m).start()
+
+            @pl.when(next_ahead == 1)
+            def _():
+                for m in range(width // cw):
+                    to_partner(i - 1, m).wait_send()
+                rows_in(i + 1).start()
 
             @pl.when(i > 0)
             def _():
-                for m in range(width // cw):
-                    to_partner(m).wait_send()
-
-            @pl.when(i == 0)
-            def _():
-                mine.start()
-
-            @pl.when(i > 0)
-            def _():
-                arrived.start()
-                pl.semaphore_wait(room, 1)
                 meta_wait(lin(xs, ys, c))
 
-            arrived.wait()
-            for m in range(width // cw):
-                to_partner(m).start()
             hot = one_hot(lin(xs, ys, c))
             step = min(512, width)
             for lo in range(0, width, step):
-                got = lax.dot_general(hot, tb[:, lo:lo + step], (((0,), (0,)), ((), ())), preferred_element_type=F32)
+                got = lax.dot_general(hot, tb[i % 2, :, lo:lo + step], (((0,), (0,)), ((), ())), preferred_element_type=F32)
                 xg[:, 0, :, lo:lo + step] = got.astype(BF16).reshape(el, per, step)
             meta_wait(lin(xs, ys, 1 - c))
             hot = one_hot(lin(xs, ys, 1 - c))
             for m in range(width // cw):
-                to_partner(m).wait_recv()
+                to_partner(i, m).wait_recv()
                 got = lax.dot_general(hot, o3[m * rows:(m + 1) * rows, :], (((0,), (0,)), ((), ())), preferred_element_type=F32)
                 xg[:, 1, :, m * cw:(m + 1) * cw] = got.astype(BF16).reshape(el, per, cw)
 
             @pl.when(i < 15)
             def _():
                 pl.semaphore_signal(room, inc=1, device_id=dev_p, device_id_type=MESH)
+
+            @pl.when(next_ahead == 1)
+            def _():
+                rows_in(i + 1).wait()
+                pl.semaphore_wait(room, 1)
+                for m in range(width // cw):
+                    to_partner(i + 1, m).start()
 
             @pl.when(i == 0)
             def _():
@@ -421,15 +448,16 @@
             return carry
 
         lax.fori_loop(0, 16, batch, 0)
-        for m in range(width // cw):
-            to_partner(m).wait_send()
+        for i in (14, 15):
+            for m in range(width // cw):
+                to_partner(i, m).wait_send()
         store(15).wait()
 
     pl.run_scoped(
         phase_one,
         pltpu.VMEM((el, ff, width), BF16),
         pltpu.VMEM((el, ff, width), BF16),
-        pltpu.VMEM((rows, width), BF16),
+        pltpu.VMEM((2, rows, width), BF16),
         pltpu.VMEM((el, 2, per, width), BF16),
         pltpu.VMEM((2,) + h_ref.shape[4:], BF16),
         pltpu.VMEM((el, 2 * per, rest), F32),
@@ -758,7 +786,7 @@
                 dma((ny * eps,)), dma((ny * eps,)),
                 dma((4,)), dma((4,)),
                 dma((4, 4)), dma((4, 4)),
-                dma((width // cw,)), dma((width // cw,)), pltpu.SemaphoreType.REGULAR,
+                dma((2, width // cw)), dma((width // cw,)), pltpu.SemaphoreType.REGULAR,
                 pltpu.VMEM((12 * pairs, cw), BF16),
                 dma((16,)), dma((16,)), dma((16,)), dma((16,)),
             ] + [dma((CHUNKS, PIECES))] * 6 + [

time: 473 us -> 475 us (level)
  no operation moved by 1% of the time
where the time goes in v9:
time: 475 us
  Pallas kernels  471 us (99%)
    pallas_call x1, Pallas kernels, local_moe(): pl.pallas_call(functools.partial(moe_kernel, nx, ny), name='moe_kernel',...  471 us

profile of v9, /device:TPU:97, one launch (start us, length us, event | category | flops | bytes accessed | tf_op | source)
XLA Modules:
  0.0 474.6 jit_solution(5584741019130839235)
XLA Ops:
  0.0 471.4 %moe_kernel.1 = (bf16[512,2048]{1,0:T(8,128)(2,1)}, bf16[4,4,2,512,2048]{4,3,2,1,0:T(8,128)(2,1)}, bf16[4,4,4,2,11,48,256]{6,5,4,3,2,1,0:T(8,128)(2,1)}, bf16[4,4,8,352,256]{4,3,2,1,0:T(8,128)(2,1)}) custom-call(bf16[512,2048]{1,0:T(8,128)(2,1)} %x_ref.1, s32[6,512]{1,0:T(8,128)} %bitcast.6, f32[6,512]{1,0:T(8,128)} %bitcast.7, ...), custom_call_target="tpu_custom_call" | custom-call | tf_op jit(solution)/shard_map/moe_kernel/pallas_call | solution.py:768
  471.4 3.2 copy.8

commit v10 on v9

--- a/solution.py
+++ b/solution.py
@@ -16,28 +16,28 @@
 
 S, A, B, O = 0, 1, 2, 3
 
-UNITS = ((2, 0), (0, 0), (1, 0), (2, 1), (0, 1), (1, 1), (2, 2), (3, 0), (1, 2), (3, 1), (0, 2), (2, 3), (3, 2), (1, 3), (0, 3), (3, 3), )
-ORDER = ((0, 0), (1, 0), (0, 1), (0, 2), (1, 1), (1, 2), (0, 3), (0, 4), (1, 3), (0, 5), (1, 4), (0, 6), (1, 5), (1, 6), (0, 7), (0, 8), (1, 7), (0, 9), (1, 8), (0, 10), (1, 9), (0, 11), (1, 10), (0, 12), (1, 11), (0, 13), (1, 12), (0, 14), (1, 13), (0, 15), (1, 14), (1, 15), )
+UNITS = ((0, 0), (1, 0), (2, 0), (0, 1), (2, 1), (1, 1), (0, 2), (3, 0), (2, 2), (3, 1), (1, 2), (2, 3), (3, 2), (0, 3), (1, 3), (3, 3), )
+ORDER = ((0, 0), (0, 1), (1, 0), (0, 2), (1, 1), (1, 2), (0, 3), (0, 4), (1, 3), (0, 5), (1, 4), (0, 6), (1, 5), (0, 7), (1, 6), (0, 8), (1, 7), (1, 8), (0, 9), (0, 10), (1, 9), (0, 11), (1, 10), (0, 12), (1, 11), (0, 13), (1, 12), (0, 14), (1, 13), (0, 15), (1, 14), (1, 15), )
 OPPOSITE_VIA_A = 4
 OPPOSITE = (2,)
-SEND_START = (('wa', 1, 0), ('wa', 2, 1), ('wb', 1, 1), ('wb', 2, 0), ('wb', 0, 1), )
+SEND_START = (('wa', 1, 0), ('wb', 0, 0), ('wb', 2, 0), )
 SEND_BEFORE = (
     (),
     (),
-    (('hd', 1), ('wa', 0, 0), ),
-    (('wf', 1, 0), ('wb', 2, 1), ('wb', 1, 0), ('wb', 0, 0), ),
+    (('hd', 1), ('wa', 2, 1), ('wa', 2, 0), ('wa', 0, 1), ('wa', 1, 1), ('wa', 0, 0), ('wf', 1, 0), ('wb', 1, 0), ('wb', 1, 1), ('wb', 0, 1), ('wb', 2, 1), ),
+    (),
+    (),
+    (),
+    (),
     (('wf', 2, 1), ),
     (),
-    (('hd', 5), ('wa', 2, 0), ('wa', 0, 1), ('wa', 1, 1), ),
-    (),
-    (('hd', 7), ),
-    (('hd', 8), ('wf', 2, 0), ),
-    (),
-    (('hf', 8), ('hd', 2), ('wf', 0, 1), ),
-    (('wf', 1, 1), ('hd', 11), ('hd', 10), ('wf', 0, 0), ),
-    (('hd', 12), ('hf', 7), ('wa', 3, 1), ),
-    (),
-    (('hf', 11), ('hf', 10), ('hd', 13), ('hd', 14), ),
+    (('hd', 8), ),
+    (('wf', 0, 1), ('hd', 7), ),
+    (('hd', 10), ),
+    (('hd', 11), ('wf', 1, 1), ('wf', 0, 0), ('wf', 2, 0), ),
+    (('hf', 7), ('hf', 10), ),
+    (('hf', 11), ('hd', 12), ('hd', 13), ),
+    (('hd', 14), ),
 )
 SEND_AFTER = (
     (),
@@ -50,26 +50,26 @@
     (),
     (),
     (),
-    (),
+    (('hf', 8), ('wa', 3, 0), ('hd', 5), ('hd', 4), ),
     (),
     (),
     (),
     (),
     (),
 )
-SEND_END = (('hd', 15), ('wb', 3, 1), ('wf', 3, 1), ('wb', 3, 0), ('lw', 0), ('lw', 1), ('lw', 2), )
+SEND_END = (('hd', 15), ('wb', 3, 1), ('wb', 3, 0), ('wf', 3, 0), ('lw', 0), ('lw', 1), ('lw', 2), )
 SEND_MAKE = (
     (),
-    (('hf', 15), ('wa', 3, 0), ('hd', 4), ('hd', 0), ('hd', 3), ),
-    (),
-    (),
-    (),
-    (('wf', 3, 0), ('hd', 6), ('hd', 9), ),
+    (('hf', 14), ),
+    (('hf', 15), ('wa', 3, 1), ('hd', 2), ('hd', 0), ('hd', 3), ),
+    (),
+    (),
+    (),
     (),
     (('lw', 3), ),
-    (('hf', 6), ),
-    (),
-    (),
+    (),
+    (),
+    (('hf', 9), ),
     (),
     (),
     (),
@@ -77,15 +77,15 @@
     (),
 )
 SEND_JOIN = (
-    (('hf', 14), ),
-    (),
-    (),
-    (),
-    (),
-    (),
-    (),
-    (),
-    (('hf', 9), ),
+    (),
+    (),
+    (),
+    (),
+    (('wf', 3, 1), ('hd', 6), ('hd', 9), ),
+    (),
+    (),
+    (('hf', 6), ),
+    (),
     (),
     (),
     (),

time: 475 us -> 471 us (level)
  Pallas kernels: 471 us -> 465 us
    pallas_call x1, Pallas kernels: 471 us -> 465 us  [local_moe(): pl.pallas_call(functools.partial(moe_kernel, nx, ny), name='moe_kernel',...]
where the time goes in v10:
time: 471 us; the launch traced here: 468 us
  Pallas kernels  465 us (99%)
    pallas_call x1, Pallas kernels, local_moe(): pl.pallas_call(functools.partial(moe_kernel, nx, ny), name='moe_kernel',...  465 us

profile of v10, /device:TPU:97, one launch (start us, length us, event | category | flops | bytes accessed | tf_op | source)
XLA Modules:
  0.0 467.8 jit_solution(13203819978735605309)
XLA Ops:
  0.0 464.7 %moe_kernel.1 = (bf16[512,2048]{1,0:T(8,128)(2,1)}, bf16[4,4,2,512,2048]{4,3,2,1,0:T(8,128)(2,1)}, bf16[4,4,4,2,11,48,256]{6,5,4,3,2,1,0:T(8,128)(2,1)}, bf16[4,4,8,352,256]{4,3,2,1,0:T(8,128)(2,1)}) custom-call(bf16[512,2048]{1,0:T(8,128)(2,1)} %x_ref.1, s32[6,512]{1,0:T(8,128)} %bitcast.6, f32[6,512]{1,0:T(8,128)} %bitcast.7, ...), custom_call_target="tpu_custom_call" | custom-call | tf_op jit(solution)/shard_map/moe_kernel/pallas_call | solution.py:768
  464.7 3.2 copy.8

commit v11 on v10

--- a/solution.py
+++ b/solution.py
@@ -16,28 +16,29 @@
 
 S, A, B, O = 0, 1, 2, 3
 
-UNITS = ((0, 0), (1, 0), (2, 0), (0, 1), (2, 1), (1, 1), (0, 2), (3, 0), (2, 2), (3, 1), (1, 2), (2, 3), (3, 2), (0, 3), (1, 3), (3, 3), )
-ORDER = ((0, 0), (0, 1), (1, 0), (0, 2), (1, 1), (1, 2), (0, 3), (0, 4), (1, 3), (0, 5), (1, 4), (0, 6), (1, 5), (0, 7), (1, 6), (0, 8), (1, 7), (1, 8), (0, 9), (0, 10), (1, 9), (0, 11), (1, 10), (0, 12), (1, 11), (0, 13), (1, 12), (0, 14), (1, 13), (0, 15), (1, 14), (1, 15), )
+SPLIT = (14, 15)
+UNITS = ((1, 0), (0, 0), (2, 0), (0, 1), (1, 1), (2, 1), (1, 2), (3, 0), (2, 2), (3, 1), (0, 2), (2, 3), (3, 2), (1, 3), (0, 3), (3, 3), )
+ORDER = ((0, 0), (1, 0), (0, 1), (0, 2), (1, 1), (1, 2), (0, 3), (0, 4), (1, 3), (0, 5), (1, 4), (0, 6), (1, 5), (0, 7), (1, 6), (0, 8), (1, 7), (1, 8), (0, 9), (0, 10), (1, 9), (0, 11), (1, 10), (0, 12), (1, 11), (0, 13), (1, 12), (0, 14), (1, 13), (0, 15), (1, 14), (1, 15), )
 OPPOSITE_VIA_A = 4
 OPPOSITE = (2,)
-SEND_START = (('wa', 1, 0), ('wb', 0, 0), ('wb', 2, 0), )
+SEND_START = (('wa', 1, 1), ('wb', 0, 0), ('wb', 2, 0), ('wb', 1, 1), ('wb', 3, 1), )
 SEND_BEFORE = (
     (),
     (),
-    (('hd', 1), ('wa', 2, 1), ('wa', 2, 0), ('wa', 0, 1), ('wa', 1, 1), ('wa', 0, 0), ('wf', 1, 0), ('wb', 1, 0), ('wb', 1, 1), ('wb', 0, 1), ('wb', 2, 1), ),
-    (),
-    (),
-    (),
-    (),
-    (('wf', 2, 1), ),
-    (),
-    (('hd', 8), ),
-    (('wf', 0, 1), ('hd', 7), ),
-    (('hd', 10), ),
-    (('hd', 11), ('wf', 1, 1), ('wf', 0, 0), ('wf', 2, 0), ),
-    (('hf', 7), ('hf', 10), ),
-    (('hf', 11), ('hd', 12), ('hd', 13), ),
-    (('hd', 14), ),
+    (('hd', 1), ('wa', 1, 0), ('wa', 0, 1), ('wa', 2, 0), ('wa', 3, 0), ('wf', 1, 1), ('wb', 1, 0), ('wb', 2, 1), ),
+    (),
+    (),
+    (),
+    (('hd', 5), ('wa', 0, 0), ('hd', 2), ),
+    (('wf', 1, 0), ),
+    (('wf', 0, 1), ),
+    (('hd', 8), ('wb', 0, 1), ),
+    (),
+    (('hf', 8), ('wa', 2, 1), ('hd', 10), ),
+    (('hd', 11), ('hd', 7), ('wf', 2, 0), ('wf', 0, 0), ),
+    (('hd', 12), ),
+    (('hf', 11), ),
+    (('hd', 14, 1), ('hd', 14, 0), ('wf', 2, 1), ),
 )
 SEND_AFTER = (
     (),
@@ -50,18 +51,18 @@
     (),
     (),
     (),
-    (('hf', 8), ('wa', 3, 0), ('hd', 5), ('hd', 4), ),
-    (),
-    (),
-    (),
-    (),
+    (),
+    (),
+    (),
+    (('hf', 10), ),
+    (('hf', 7), ('hd', 13), ),
     (),
 )
-SEND_END = (('hd', 15), ('wb', 3, 1), ('wb', 3, 0), ('wf', 3, 0), ('lw', 0), ('lw', 1), ('lw', 2), )
+SEND_END = (('hf', 14, 1), ('hd', 15, 1), ('hd', 15, 0), ('wb', 3, 0), ('wf', 3, 0), ('lw', 0), ('lw', 1), )
 SEND_MAKE = (
     (),
-    (('hf', 14), ),
-    (('hf', 15), ('wa', 3, 1), ('hd', 2), ('hd', 0), ('hd', 3), ),
+    (('lw', 2), ),
+    (('hf', 15, 1), ),
     (),
     (),
     (),
@@ -77,8 +78,8 @@
     (),
 )
 SEND_JOIN = (
-    (),
-    (),
+    (('hf', 14, 0), ),
+    (('hf', 15, 0), ('wa', 3, 1), ('hd', 4), ('hd', 0), ('hd', 3), ),
     (),
     (),
     (('wf', 3, 1), ('hd', 6), ('hd', 9), ),
@@ -265,15 +266,24 @@
         block = w_ref.at[k, ya, pl.ds(g * ep_piece, ep_piece)]
         return remote(block, block, wf_s.at[k, g], wf_r.at[k, g], dev_b)
 
-    def hd(i):
+    def hd(i, s=None):
         dxm, q = order_of(i)
         block = h_ref.at[y, (x + dxm) % nx, yq[q]]
-        return remote(block, block, hd_s.at[i], hd_r.at[i], dev_a if q < 2 else dev_b)
-
-    def hf(i):
+        at = i
+        if s is not None:
+            block, at = block.at[either(s)], 16 * s + i
+        return remote(block, block, hd_s.at[at], hd_r.at[at], dev_a if q < 2 else dev_b)
+
+    def hf(i, s=None):
         dxm, q = order_of(i)
         block = h_ref.at[yb, (x + dxm) % nx, place(yb, q)]
-        return remote(block, block, hf_s.at[i], hf_r.at[i], dev_a)
+        at = i
+        if s is not None:
+            block, at = block.at[either(s)], 16 * s + i
+        return remote(block, block, hf_s.at[at], hf_r.at[at], dev_a)
+
+    def messages(i):
+        return ((i, 0), (i, 1)) if i in SPLIT else ((i,),)
 
     def send(actions, load_w=None):
         for action in actions:
@@ -483,9 +493,10 @@
                 wb(k, g).wait_send()
                 wf(k, g).wait_send()
         for i in range(16):
-            hd(i).wait_send()
-            if order_of(i)[1] >= 2:
-                hf(i).wait_send()
+            for message in messages(i):
+                hd(*message).wait_send()
+                if order_of(i)[1] >= 2:
+                    hf(*message).wait_send()
 
     def window(e):
         return e * rest // 128 * 128, -(-(e + 1) * rest // 128) * 128
@@ -548,10 +559,9 @@
 
         def first_use(j):
             minus, plus = (3 - j) % 4, (1 + j) % 4
-            hd(BATCH[(minus, A)]).wait_recv()
-            hd(BATCH[(plus, S)]).wait_recv()
-            hf(BATCH[(minus, O)]).wait_recv()
-            hf(BATCH[(plus, B)]).wait_recv()
+            for copy, block in ((hd, (minus, A)), (hd, (plus, S)), (hf, (minus, O)), (hf, (plus, B))):
+                for message in messages(BATCH[block]):
+                    copy(*message).wait_recv()
 
         def partner_copy(n, d):
             return remote(pp.at[n % 2, d], db.at[n % 2, d], pp_s.at[n % 2, d], db_r.at[n % 2, d], dev_p)
@@ -788,7 +798,7 @@
                 dma((4, 4)), dma((4, 4)),
                 dma((2, width // cw)), dma((width // cw,)), pltpu.SemaphoreType.REGULAR,
                 pltpu.VMEM((12 * pairs, cw), BF16),
-                dma((16,)), dma((16,)), dma((16,)), dma((16,)),
+                dma((32,)), dma((32,)), dma((32,)), dma((32,)),
             ] + [dma((CHUNKS, PIECES))] * 6 + [
                 dma((2, CHUNKS, 3)), dma((2, 2)), dma((CHUNKS,)),
                 pltpu.SemaphoreType.REGULAR,

time: 471 us -> 471 us (level)
  no operation moved by 1% of the time
where the time goes in v11:
time: 471 us; the launch traced here: 468 us
  Pallas kernels  465 us (99%)
    pallas_call x1, Pallas kernels, local_moe(): pl.pallas_call(functools.partial(moe_kernel, nx, ny), name='moe_kernel',...  465 us

profile of v11, /device:TPU:97, one launch (start us, length us, event | category | flops | bytes accessed | tf_op | source)
XLA Modules:
  0.0 468.4 jit_solution(16765408031658002030)
XLA Ops:
  0.0 465.3 %moe_kernel.1 = (bf16[512,2048]{1,0:T(8,128)(2,1)}, bf16[4,4,2,512,2048]{4,3,2,1,0:T(8,128)(2,1)}, bf16[4,4,4,2,11,48,256]{6,5,4,3,2,1,0:T(8,128)(2,1)}, bf16[4,4,8,352,256]{4,3,2,1,0:T(8,128)(2,1)}) custom-call(bf16[512,2048]{1,0:T(8,128)(2,1)} %x_ref.1, s32[6,512]{1,0:T(8,128)} %bitcast.6, f32[6,512]{1,0:T(8,128)} %bitcast.7, ...), custom_call_target="tpu_custom_call" | custom-call | tf_op jit(solution)/shard_map/moe_kernel/pallas_call | solution.py:778
  465.3 3.2 copy.8
